TPU v7x, 32 devices: a whole 2x2x4 slice. The times are simulated.
32 devices in a mesh: ell: 4 (over y, x), blk: 8 (over z, core).
Axes of the slice: x: 2, y: 2, z: 4, core: 2. Of those that a mesh axis runs over, the one named last changes fastest.
Arguments:
- wigner: bfloat16 [8, 17, 2101248], P(None, None, ('ell', 'blk')), may hold values from -6 to 6
- sky_alm: float32 [2, 2101248], P(None, ('ell', 'blk')), may hold values from -0.03125 to 0.03125
- beam_blm: float32 [2, 17, 2048], replicated, may hold values from -4.25 to 4.25
- slot_col: int32 [2101248], P(('ell', 'blk')), may hold values from -1 to 255, as said below
- slot_ell: int32 [2101248], P(('ell', 'blk')), may hold values from 0 to 2047, as said below
- order_of_column: int32 [2048], replicated, may hold values from 0 to 2047, as said below
Outputs:
- conv_cube: float32 [8, 32, 4096], P('ell', 'blk')
Inputs may be any that keep to these rules, and one draw needn't show every extreme that they name: `slot_col`: slot block b (slots b * 65664 to b * 65664 + 65663) belongs to ell index b // 8 and blk index b % 8; at most 65568 slots of a block are live, and some blocks have exactly that many. `slot_ell`: every pair (l, m) with m <= l < 2048 stands in exactly one live slot; within a blk group, higher ell indices hold degrees no lower than those of lower ell indices. `order_of_column`: A permutation of 0 to 2047; every blk group's orders hold the same number of pairs.
All inputs are finite; a program needn't handle non-finite values.
Results may differ from a plain program's by a relative error of at most 0.0029.
Values sent between devices are 32-bit elements; how exact they have to be, the bound alone decides.
No kernel may reach another device: no remote copies, remote signals or barrier semaphores. Data moves between devices by JAX's collectives and lax.ppermute only.
A program may use at most 256 MiB of HBM per device.

v0:
```python
import math

import jax
import jax.numpy as jnp
from jax import lax
from jax.sharding import PartitionSpec as P

NPSI = 32


def phase_table(rows, cols, period):
    product = (
        jnp.arange(rows, dtype=jnp.int32)[:, None]
        * jnp.arange(cols, dtype=jnp.int32)[None, :]
        % period
    )
    angle = product.astype(jnp.float32) * (2.0 * math.pi / period)
    return (jnp.cos(angle), jnp.sin(angle))


def psi_table(order_count, samples):
    cosines, sine_terms = phase_table(order_count, samples, samples)
    real_row = jnp.stack([cosines, sine_terms], axis=1)
    imag_row = jnp.stack([-sine_terms, cosines], axis=1)
    return jnp.stack([real_row, imag_row], axis=0)


def to_psi(harmonic, table):
    return jnp.einsum("trkc,rksp->tspc", harmonic, table, precision=lax.Precision.HIGHEST)


def to_phi(fields, order_of_column):
    cycles = fields.shape[0]
    samples = fields.shape[2]
    degrees = fields.shape[3]
    period = 2 * degrees
    inner = 2 ** ((period.bit_length() - 1) // 2)
    outer = period // inner
    highest = lax.Precision.HIGHEST
    high_part = order_of_column // inner
    low_part = order_of_column % inner
    turns = high_part[:, None] * jnp.arange(outer, dtype=jnp.int32)[None, :] % outer
    angle = turns.astype(jnp.float32) * (2.0 * math.pi / outer)
    cos_first = jnp.cos(angle)
    sin_first = jnp.sin(angle)
    select = (low_part[:, None] == jnp.arange(inner, dtype=jnp.int32)[None, :]).astype(jnp.float32)
    real_in = fields[:, 0]
    imag_in = fields[:, 1]
    weighted_re = real_in[..., None] * cos_first - imag_in[..., None] * sin_first
    weighted_im = real_in[..., None] * sin_first + imag_in[..., None] * cos_first
    first_re = jnp.einsum("tpcj,cv->tpvj", weighted_re, select, precision=highest)
    first_im = jnp.einsum("tpcj,cv->tpvj", weighted_im, select, precision=highest)
    cos_twist, sin_twist = phase_table(inner, outer, period)
    twist_re = first_re * cos_twist - first_im * sin_twist
    twist_im = first_re * sin_twist + first_im * cos_twist
    cos_last, sin_last = phase_table(inner, inner, inner)
    result = jnp.einsum("tpvj,vw->tpwj", twist_re, cos_last, precision=highest) - jnp.einsum(
        "tpvj,vw->tpwj", twist_im, sin_last, precision=highest
    )
    return result.reshape(cycles, samples, period)


def on_device(wigner, sky_alm, beam_blm, slot_col, slot_ell, order_of_column):
    cycle_total = wigner.shape[0]
    order_count = wigner.shape[1]
    slot_count = wigner.shape[2]
    ell_count = lax.axis_size("ell")
    blk_count = lax.axis_size("blk")
    col_count = order_of_column.shape[0] // blk_count
    cycle_share = cycle_total // ell_count
    degree_count = beam_blm.shape[2]
    beam_rows = beam_blm.reshape(2 * order_count, degree_count).T
    picked = jnp.take(beam_rows, slot_ell, axis=0)
    beam_slots = picked.T.reshape(2, order_count, slot_count)
    coeffs = jnp.stack(
        [
            sky_alm[0] * beam_slots[0] - sky_alm[1] * beam_slots[1],
            sky_alm[0] * beam_slots[1] + sky_alm[1] * beam_slots[0],
        ]
    )
    one_hot = (slot_col[:, None] == jnp.arange(col_count, dtype=jnp.int32)[None, :]).astype(
        jnp.bfloat16
    )
    table = psi_table(order_count, NPSI)
    values = (wigner[:, None].astype(jnp.float32) * coeffs[None]).astype(jnp.bfloat16)
    col_sums = jnp.dot(values.reshape(-1, slot_count), one_hot, preferred_element_type=jnp.float32)
    summed = lax.psum_scatter(
        col_sums.reshape(cycle_share * lax.axis_size("ell"), 2, order_count, col_count),
        "ell",
        scatter_dimension=0,
        tiled=True,
    )
    owned = to_psi(summed, table)
    return to_phi(
        lax.all_to_all(owned, "blk", split_axis=2, concat_axis=3, tiled=True), order_of_column
    )


def solution(mesh):
    return jax.shard_map(
        on_device,
        mesh=mesh,
        in_specs=(
            P(None, None, ("ell", "blk")),
            P(None, ("ell", "blk")),
            P(),
            P(("ell", "blk")),
            P(("ell", "blk")),
            P(),
        ),
        out_specs=P("ell", "blk", None),
        check_vma=False,
    )
```

profile of v0, /device:TPU:0, one launch (start us, length us, event | category | flops | bytes accessed | tf_op | source)
XLA Modules:
  0.0 433.9 jit_solution(10651891721096126606)
XLA Ops:
  6.5 0.0 reduce-scatter.2.cloned.1.call-start
  6.5 1.0 compare_select_fusion
  7.5 1.0 compare_and_fusion
  8.6 2.7 slice_reduce_fusion.1
  11.2 1.1 copy.43
  12.4 0.4 copy.44
  12.8 120.9 %gather_fusion = f32[65664,34]{1,0:T(8,128)} fusion(f32[2048,34]{1,0:T(8,128)S(1)} %bitcast.72, s32[66560]{0:T(1024)S(1)} %pad_clamp_fusion), kind=kCustom, calls=%fused_computation | custom fusion | bytes 18123264 | tf_op jit(solution)/shard_map/jit(_take)/gather | solution.py:73
  133.7 36.4 %select_bitcast_fusion = f32[34,65664]{0,1:T(8,128)} fusion(f32[65664,34]{1,0:T(8,128)} %gather_fusion, pred[65664]{0:T(1024)(128)(4,1)S(1)} %compare_and_fusion), kind=kLoop, calls=%fused_computation.11 | loop fusion | flops 2232576 | bytes 17926272 | tf_op jit(solution)/shard_map/jit(_take)/select_n | solution.py:73
  170.1 45.0 %subtract_bitcast_fusion = (f32[1,17,65664]{1,2,0:T(8,128)}, f32[1,17,65664]{1,2,0:T(8,128)}) fusion(f32[34,65664]{0,1:T(8,128)} %select_bitcast_fusion, f32[65664]{0:T(1024)S(1)} %get-tuple-element.6, f32[65664]{0:T(1024)S(1)} %get-tuple-element.5), kind=kLoop, calls=%fused_computation.10 | loop fusion | flops 6697728 | bytes 18385920 | tf_op jit(solution)/shard_map/stack | solution.py:75
  215.1 44.3 %pad_maximum_fusion = f32[2,17,65664]{1,2,0:T(8,128)} fusion(f32[1,17,65664]{1,2,0:T(8,128)} %get-tuple-element.8, f32[1,17,65664]{1,2,0:T(8,128)} %get-tuple-element.7), kind=kLoop, calls=%fused_computation.2 | loop fusion | flops 2232576 | bytes 17860608 | tf_op jit(solution)/shard_map/stack | solution.py:75
  259.4 38.5 %copy.45 = f32[2,17,65664]{2,1,0:T(8,128)} copy(f32[2,17,65664]{1,2,0:T(8,128)} %pad_maximum_fusion) | data formatting | bytes 17860608 | tf_op jit(solution)/shard_map/stack | solution.py:75
  297.8 0.0 copy-start
  297.8 22.0 %copy.42 = f32[8,17,65664]{2,1,0:T(8,128)} copy(bf16[8,17,65664]{2,0,1:T(8,128)(2,1)} %param.6) | data formatting | bytes 53581824 | tf_op jit(solution)/shard_map/convert_element_type | solution.py:85
  319.9 0.0 copy-done
  319.9 30.2 %fusion.94 = pred[65664,256,1,1]{1,0,3,2:T(32,128)(4,1)S(1)} fusion(s32[65664]{0:T(1024)S(1)} %copy-done), kind=kLoop, calls=%fused_computation.4.clone.clone.2 | loop fusion | flops 16809984 | bytes 17072640 | tf_op jit(solution)/shard_map/dot_general | solution.py:86
  350.1 0.0 copy-start.1
  350.1 27.0 %fusion.1 = f32[8,2,17,256]{3,2,1,0:T(8,128)} fusion(f32[2,17,65664]{2,1,0:T(8,128)} %copy.45, f32[8,17,65664]{2,1,0:T(8,128)} %copy.42, pred[65664,256,1,1]{1,0,3,2:T(32,128)(4,1)S(1)} %fusion.94), kind=kOutput, calls=%fused_computation.5 | convolution fusion | flops 9180352512 | bytes 61740032 | tf_op jit(solution)/shard_map/dot_general | solution.py:86
  377.0 0.0 reduce-scatter.2.cloned.1.call-update
  377.1 0.1 fusion.80
  377.1 0.1 fusion.78
  377.2 0.0 copy-done.1
  377.3 27.4 %reduce-scatter.2.cloned.1.call-done = f32[2,2,17,256]{3,2,1,0:T(8,128)} async-done(((f32[8,2,17,256]{3,2,1,0:T(8,128)}), f32[2,2,17,256]{3,2,1,0:T(8,128)}) %reduce-scatter.2.cloned.1.call-update) | async-done | bytes 69648 | tf_op jit(solution)/shard_map/reduce_scatter | solution.py:87
  404.7 1.2 convolution_bitcast_fusion
  405.9 0.8 copy.46
  406.7 4.6 %all-to-all-start = ((f32[2,2,32,256]{3,0,1,2:T(2,128)}), f32[2,2,32,256]{3,0,1,2:T(2,128)S(1)}, u32[]{:S(2)}, u32[]{:S(2)}) async-start(f32[2,2,32,256]{3,0,1,2:T(2,128)} %copy.46), calls=%async_computation.1 | async-start | bytes 262144 | tf_op jit(solution)/shard_map/all_to_all | solution.py:95
  411.2 2.0 fusion.42
  413.3 0.1 fusion.68
  413.4 0.1 copy.48
  413.5 0.2 fusion.67
  413.7 0.1 copy.49
  413.7 4.3 all-to-all-done
  418.0 0.1 copy.57
  418.1 0.1 all_to_all.16
  418.2 3.5 fusion.10
  421.6 3.5 fusion.6
  425.1 0.5 fusion.33
  425.7 0.5 fusion.22
  426.2 0.8 reshape.187
  (5 shorter events, 0.1 us)
Async XLA Ops:
  6.5 398.1 %reduce-scatter.2.cloned.1.call-start = ((), (), s32[]{:S(2)}) async-start(), calls=%async_computation.2 | async-start | bytes 491520 | tf_op jit(solution)/shard_map/reduce_scatter | solution.py:87
  297.8 22.0 %copy-start = (s32[65664]{0:T(1024)S(1)}, s32[65664]{0:T(1024)}, u32[]{:S(2)}) copy-start(s32[65664]{0:T(1024)} %param.9) | copy-start | bytes 787972
  350.1 27.2 %copy-start.1 = (s32[2048]{0:T(1024)S(1)}, s32[2048]{0:T(1024)}, u32[]{:S(2)}) copy-start(s32[2048]{0:T(1024)} %param.11) | copy-start | bytes 24580
  406.7 11.3 %all-to-all-start = ((f32[2,2,32,256]{3,0,1,2:T(2,128)}), f32[2,2,32,256]{3,0,1,2:T(2,128)S(1)}, u32[]{:S(2)}, u32[]{:S(2)}) async-start(f32[2,2,32,256]{3,0,1,2:T(2,128)} %copy.46), calls=%async_computation.1 | async-start | bytes 262144 | tf_op jit(solution)/shard_map/all_to_all | solution.py:95
Sparse Core Ops, SparseCore 0:
  377.2 27.4 reduce-scatter.1
where the time goes:
time: 435 us; the launch traced here: 434 us
  local copies, waits for them, and re-layouts  187 us (43%)
  other arithmetic  160 us (37%)
  matrix products  36.2 us (8%)
  waiting for transfers between devices  31.7 us (7%)
  between operations  13.5 us (3%)
  starting transfers between devices  4.59 us (1%)
    gather x1, local copies, waits for them, and re-layouts, on_device(): picked = jnp.take(beam_rows, slot_ell, axis=0)  121 us
    another operation x2, other arithmetic, on_device(): jnp.stack([sky_alm[0] * beam_slots[0] - sky_alm[1] * beam_slots[1], sky_a...  89.3 us
    another operation x1, local copies, waits for them, and re-layouts, on_device(): jnp.stack([sky_alm[0] * beam_slots[0] - sky_alm[1] * beam_slots[1], sky_a...  38.5 us
    select_n x2, other arithmetic, on_device(): picked = jnp.take(beam_rows, slot_ell, axis=0)  37.4 us
    dot_general x1, other arithmetic, on_device(): jnp.dot(values.reshape(-1, slot_count), one_hot, preferred_element_type=j...  30.2 us
    reduce_scatter x1, waiting for transfers between devices, on_device(): lax.psum_scatter(col_sums.reshape(cycle_share * lax.axis_size('ell'), 2,...  27.4 us
    dot_general x1, matrix products, on_device(): jnp.dot(values.reshape(-1, slot_count), one_hot, preferred_element_type=j...  27 us
    convert_element_type x1, local copies, waits for them, and re-layouts, on_device(): wigner[:, None].astype(jnp.float32) * coeffs[None]  22 us
  transfers between devices with their start and end apart: 2, of which 2 were waited for; matrix products, arithmetic and copies ran while one was open for 1% of the time, Pallas kernels for 0%

commit v1 on v0

--- a/solution.py
+++ b/solution.py
@@ -1,11 +1,18 @@
+import functools
 import math
 
 import jax
 import jax.numpy as jnp
 from jax import lax
+from jax.experimental import pallas as pl
+from jax.experimental.pallas import tpu as pltpu
 from jax.sharding import PartitionSpec as P
 
 NPSI = 32
+LANES = 128
+TILE = 256
+F32 = jnp.float32
+BF16 = jnp.bfloat16
 
 
 def phase_table(rows, cols, period):
@@ -60,6 +67,139 @@
     return result.reshape(cycles, samples, period)
 
 
+def sums_kernel(
+    shape, base_ref, table_ref, *refs
+):
+    (cycles, orders, cols, spans, chunk, main_steps) = shape
+    streams, (out_ref, values_ref) = refs[:-2], refs[-2:]
+    step = pl.program_id(0)
+    full = orders // 16 * 16
+    pair = 2 * full
+
+    def one_hot(row, count):
+        rows = lax.broadcasted_iota(jnp.int32, (count, row.shape[1]), 0).astype(F32).astype(BF16)
+        match = row.astype(F32).astype(BF16) == rows
+        return jnp.where(match, jnp.ones_like(rows), jnp.zeros_like(rows))
+
+    def add_chunk(w_ref, sky_ref, col_ref, ell_ref, offset, width):
+        where = pl.ds(offset, width)
+        index = ell_ref[:, where] - base_ref[0]
+        span = lax.shift_right_arithmetic(index, 8)
+        hot_ell = one_hot(lax.bitwise_and(index, TILE - 1), TILE)
+        picked = jnp.dot(table_ref[0], hot_ell, preferred_element_type=F32) + jnp.dot(
+            table_ref[1], hot_ell, preferred_element_type=F32
+        )
+        beam_re = picked[0:full]
+        beam_im = picked[full:pair]
+        for j in range(1, spans):
+            here = span == j
+            beam_re = jnp.where(here, picked[j * pair : j * pair + full], beam_re)
+            beam_im = jnp.where(here, picked[j * pair + full : (j + 1) * pair], beam_im)
+        sky_re = sky_ref[0:1, where]
+        sky_im = sky_ref[1:2, where]
+        coef_re = sky_re * beam_re - sky_im * beam_im
+        coef_im = sky_re * beam_im + sky_im * beam_re
+        rows8 = lax.broadcasted_iota(jnp.int32, (8, width), 0) == span
+        for k in range(orders):
+            if k < full:
+                row_re = coef_re[k : k + 1]
+                row_im = coef_im[k : k + 1]
+            else:
+                at = spans * pair + (k - full) * 16
+                last_re = jnp.sum(jnp.where(rows8, picked[at : at + 8], 0.0), axis=0, keepdims=True)
+                last_im = jnp.sum(
+                    jnp.where(rows8, picked[at + 8 : at + 16], 0.0), axis=0, keepdims=True
+                )
+                row_re = sky_re * last_re - sky_im * last_im
+                row_im = sky_re * last_im + sky_im * last_re
+            w = w_ref[k, :, where].astype(F32)
+            both = jnp.concatenate([w * row_re, w * row_im], axis=0).astype(BF16)
+            values_ref[k * 2 * cycles : (k + 1) * 2 * cycles, 0:width] = both
+        hot_col = one_hot(col_ref[:, where], cols)
+        out_ref[...] += lax.dot_general(
+            values_ref[:, 0:width],
+            hot_col,
+            (((1,), (1,)), ((), ())),
+            preferred_element_type=F32,
+        )
+
+    @pl.when(step == 0)
+    def _():
+        out_ref[...] = jnp.zeros_like(out_ref)
+
+    main = streams[:4]
+    block = main[0].shape[2]
+
+    def body(i, carry):
+        add_chunk(*main, pl.multiple_of(i * chunk, chunk), chunk)
+        return carry
+
+    lax.fori_loop(0, block // chunk, body, 0)
+
+    if len(streams) > 4:
+
+        @pl.when(step == main_steps - 1)
+        def _():
+            add_chunk(*streams[4:], 0, streams[4].shape[2])
+
+
+def column_sums(wigner, sky_alm, table, base, slot_col, slot_ell, cols, spans):
+    orders, cycles, slots = wigner.shape
+    block = 4096
+    chunk = 512
+    steps = slots // block
+    tail = slots - steps * block
+    rows = 2 * orders * cycles
+
+    def specs(width, at):
+        return [
+            pl.BlockSpec((orders, cycles, width), lambda i, b: (0, 0, at(i))),
+            pl.BlockSpec((2, width), lambda i, b: (0, at(i))),
+            pl.BlockSpec((1, width), lambda i, b: (0, at(i))),
+            pl.BlockSpec((1, width), lambda i, b: (0, at(i))),
+        ]
+
+    arrays = [wigner, sky_alm, slot_col, slot_ell]
+    in_specs = [pl.BlockSpec(table.shape, lambda i, b: (0, 0, 0))] + specs(block, lambda i: i)
+    operands = [table] + arrays
+    if tail:
+        at = slots // tail - 1
+        in_specs += specs(tail, lambda i: at)
+        operands += arrays
+    return pl.pallas_call(
+        functools.partial(sums_kernel, (cycles, orders, cols, spans, chunk, steps)),
+        grid_spec=pltpu.PrefetchScalarGridSpec(
+            num_scalar_prefetch=1,
+            grid=(steps,),
+            in_specs=in_specs,
+            out_specs=pl.BlockSpec((rows, cols), lambda i, b: (0, 0)),
+            scratch_shapes=[pltpu.VMEM((rows, chunk), BF16)],
+        ),
+        out_shape=jax.ShapeDtypeStruct((rows, cols), F32),
+        compiler_params=pltpu.CompilerParams(dimension_semantics=("arbitrary",)),
+        name="column_sums",
+    )(base, *operands)
+
+
+def beam_table(beam_blm, base, spans):
+    orders = beam_blm.shape[1]
+    full = orders // 16 * 16
+    window = lax.dynamic_slice_in_dim(beam_blm, base, spans * TILE, axis=2)
+    window = window.reshape(2, orders, spans, TILE)
+    head = window[:, :full].transpose(2, 0, 1, 3).reshape(spans * 2 * full, TILE)
+    rest = window[:, full:].transpose(1, 0, 2, 3)
+    rest = jnp.pad(rest, ((0, 0), (0, 0), (0, 8 - spans), (0, 0)))
+    rows = jnp.concatenate([head, rest.reshape(-1, TILE)], axis=0)
+    upper = lax.reduce_precision(rows, exponent_bits=8, mantissa_bits=7)
+    return jnp.stack([upper.astype(BF16), (rows - upper).astype(BF16)])
+
+
+def degree_width(degrees, ell_count, blk_count, cols):
+    live = degrees * (degrees + 1) // 2 // (ell_count * blk_count)
+    width = degrees - (ell_count - 1) * live // cols
+    return min(degrees, -(-width // TILE) * TILE)
+
+
 def on_device(wigner, sky_alm, beam_blm, slot_col, slot_ell, order_of_column):
     cycle_total = wigner.shape[0]
     order_count = wigner.shape[1]
@@ -69,28 +209,24 @@
     col_count = order_of_column.shape[0] // blk_count
     cycle_share = cycle_total // ell_count
     degree_count = beam_blm.shape[2]
-    beam_rows = beam_blm.reshape(2 * order_count, degree_count).T
-    picked = jnp.take(beam_rows, slot_ell, axis=0)
-    beam_slots = picked.T.reshape(2, order_count, slot_count)
-    coeffs = jnp.stack(
-        [
-            sky_alm[0] * beam_slots[0] - sky_alm[1] * beam_slots[1],
-            sky_alm[0] * beam_slots[1] + sky_alm[1] * beam_slots[0],
-        ]
-    )
-    one_hot = (slot_col[:, None] == jnp.arange(col_count, dtype=jnp.int32)[None, :]).astype(
-        jnp.bfloat16
-    )
-    table = psi_table(order_count, NPSI)
-    values = (wigner[:, None].astype(jnp.float32) * coeffs[None]).astype(jnp.bfloat16)
-    col_sums = jnp.dot(values.reshape(-1, slot_count), one_hot, preferred_element_type=jnp.float32)
-    summed = lax.psum_scatter(
-        col_sums.reshape(cycle_share * lax.axis_size("ell"), 2, order_count, col_count),
-        "ell",
-        scatter_dimension=0,
-        tiled=True,
-    )
-    owned = to_psi(summed, table)
+    width = degree_width(degree_count, ell_count, blk_count, col_count)
+    spans = width // TILE
+    lowest = jnp.min(jnp.where(slot_col >= 0, slot_ell, degree_count))
+    base = jnp.minimum(lowest, degree_count - width)
+    col_sums = column_sums(
+        jnp.transpose(wigner, (1, 0, 2)),
+        sky_alm,
+        beam_table(beam_blm, base, spans),
+        base.reshape(1),
+        slot_col.reshape(1, slot_count),
+        slot_ell.reshape(1, slot_count),
+        col_count,
+        spans,
+    )
+    parts = col_sums.reshape(order_count, 2, cycle_total, col_count).transpose(2, 1, 0, 3)
+    parts = parts.reshape(ell_count, cycle_share, 2, order_count, col_count)
+    summed = jnp.sum(lax.all_to_all(parts, "ell", split_axis=0, concat_axis=0, tiled=True), axis=0)
+    owned = to_psi(summed, psi_table(order_count, NPSI))
     return to_phi(
         lax.all_to_all(owned, "blk", split_axis=2, concat_axis=3, tiled=True), order_of_column
     )

time: 435 us -> 115 us (0.26)
  local copies, waits for them, and re-layouts: 187 us -> 7.99 us
  other arithmetic: 160 us -> 5.11 us
  Pallas kernels: 0 us -> 72.5 us
  matrix products: 36.2 us -> 8.35 us
  waiting for transfers between devices: 31.7 us -> 9.58 us
  between operations: 13.5 us -> 0.81 us
  starting transfers between devices: 4.59 us -> 10 us
    gather x1 -> x0, local copies, waits for them, and re-layouts: 121 us -> none  [on_device(): picked = jnp.take(beam_rows, slot_ell, axis=0)]
    another operation x2 -> x1, other arithmetic: 89.3 us -> 0.69 us  [beam_table(): return jnp.stack([upper.astype(BF16), (rows - upper).astype(BF16)])]
    pallas_call x0 -> x1, Pallas kernels: none -> 72.5 us  [column_sums(): pl.pallas_call(functools.partial(sums_kernel, (cycles, orders, cols, span...]
    another operation x1 -> x0, local copies, waits for them, and re-layouts: 38.5 us -> none  [on_device(): jnp.stack([sky_alm[0] * beam_slots[0] - sky_alm[1] * beam_slots[1], sky_a...]
    select_n x2 -> x0, other arithmetic: 37.4 us -> none  [on_device(): picked = jnp.take(beam_rows, slot_ell, axis=0)]
    dot_general x1 -> x0, other arithmetic: 30.2 us -> none  [on_device(): jnp.dot(values.reshape(-1, slot_count), one_hot, preferred_element_type=j...]
    reduce_scatter x1 -> x0, waiting for transfers between devices: 27.4 us -> none  [on_device(): lax.psum_scatter(col_sums.reshape(cycle_share * lax.axis_size('ell'), 2,...]
    dot_general x1 -> x0, matrix products: 27 us -> none  [on_device(): jnp.dot(values.reshape(-1, slot_count), one_hot, preferred_element_type=j...]
  transfers between devices with their start and end apart: 2 -> 2, of which waited for: 2 -> 2; matrix products, arithmetic and copies ran while one was open for 1% -> 2% of each run, Pallas kernels for 0% -> 0%
where the time goes in v1:
time: 115 us; the launch traced here: 114 us
  Pallas kernels  72.5 us (63%)
  starting transfers between devices  10 us (9%)
  waiting for transfers between devices  9.58 us (8%)
  matrix products  8.35 us (7%)
  local copies, waits for them, and re-layouts  7.99 us (7%)
  other arithmetic  5.11 us (4%)
    pallas_call x1, Pallas kernels, column_sums(): pl.pallas_call(functools.partial(sums_kernel, (cycles, orders, cols, span...  72.5 us
    all_to_all x1, waiting for transfers between devices, on_device(): lax.all_to_all(parts, 'ell', split_axis=0, concat_axis=0, tiled=True)  5.33 us
    all_to_all x1, starting transfers between devices, on_device(): lax.all_to_all(parts, 'ell', split_axis=0, concat_axis=0, tiled=True)  5.16 us
    all_to_all x1, starting transfers between devices, on_device(): lax.all_to_all(owned, 'blk', split_axis=2, concat_axis=3, tiled=True)  4.86 us
    all_to_all x1, waiting for transfers between devices, on_device(): lax.all_to_all(owned, 'blk', split_axis=2, concat_axis=3, tiled=True)  4.25 us
    dot_general x1, matrix products, to_phi(): jnp.einsum('tpcj,cv->tpvj', weighted_im, select, precision=highest)  3.48 us
    dot_general x1, matrix products, to_phi(): jnp.einsum('tpcj,cv->tpvj', weighted_re, select, precision=highest)  3.47 us
  transfers between devices with their start and end apart: 2, of which 2 were waited for; matrix products, arithmetic and copies ran while one was open for 2% of the time, Pallas kernels for 0%

profile of v1, /device:TPU:0, one launch (start us, length us, event | category | flops | bytes accessed | tf_op | source)
XLA Modules:
  0.0 114.3 jit_solution(6923430973596615732)
XLA Ops:
  0.0 0.0 copy-start
  0.0 1.8 %select_reduce_fusion = s32[]{:T(128)} fusion(s32[65664]{0:T(1024)} %param.10, s32[65664]{0:T(1024)} %param.9), kind=kLoop, calls=%fused_computation.30 | loop fusion | flops 196991 | bytes 525316 | tf_op jit(solution)/shard_map/reduce_min | solution.py:214
  2.4 0.0 copy-done
  2.5 0.2 constant_dynamic-slice_fusion
  2.7 0.1 reshape.265
  2.9 1.8 %reshape.266.refs_2_.refs_6_ = s32[1,65664]{1,0:T(1,128)} reshape(s32[65664]{0:T(1024)} %param.9) | data formatting | bytes 525312 | tf_op jit(solution)/shard_map/reshape | solution.py:221
  4.7 1.8 %reshape.267.refs_3_.refs_7_ = s32[1,65664]{1,0:T(1,128)} reshape(s32[65664]{0:T(1024)} %param.10) | data formatting | bytes 525312 | tf_op jit(solution)/shard_map/reshape | solution.py:222
  6.6 0.1 copy.23
  6.7 0.7 pad_maximum_fusion.1.table_ref
  7.4 0.0 copy-start.1
  7.4 72.5 %column_sums.1 = f32[272,256]{1,0:T(8,128)} custom-call(s32[1]{0:T(128)} %bitcast.9.base_ref, bf16[2,176,256]{2,1,0:T(8,128)(2,1)} %pad_maximum_fusion.1.table_ref, bf16[17,8,65664]{2,1,0:T(8,128)(2,1)} %bitcast.70, f32[2,65664]{1,0:T(2,128)} %refs_5_.1, s32[1,65664]{1,0:T(1,128)} %reshape.266.refs_2_.refs_6_, s32[1,65664]{1,0:T(1,128)} %reshape.267.refs_3_.refs_7_, ...), custom_call_target="tpu_custom_call" | custom-call | tf_op jit(solution)/shard_map/column_sums/pallas_call | solution.py:169
  79.9 1.1 copy.24
  81.0 0.8 copy.25
  81.8 5.2 %all-to-all-start = ((f32[4,2,2,17,256]{4,1,2,3,0:T(2,128)}), f32[4,2,2,17,256]{4,1,2,3,0:T(2,128)S(1)}, u32[]{:S(2)}, u32[]{:S(2)}) async-start(f32[4,2,2,17,256]{4,1,2,3,0:T(2,128)} %copy.25), calls=%async_computation | async-start | bytes 557056 | tf_op jit(solution)/shard_map/all_to_all | solution.py:228
  87.0 0.1 fusion.74
  87.1 0.1 fusion.76
  87.2 0.0 copy-done.1
  87.2 5.3 %all-to-all-done = f32[4,2,2,17,256]{4,1,2,3,0:T(2,128)S(1)} async-done(((f32[4,2,2,17,256]{4,1,2,3,0:T(2,128)}), f32[4,2,2,17,256]{4,1,2,3,0:T(2,128)S(1)}, u32[]{:S(2)}, u32[]{:S(2)}) %all-to-all-start) | async-done | bytes 278560 | tf_op jit(solution)/shard_map/all_to_all | solution.py:228
  92.5 0.1 reduce_sum.9
  92.6 0.3 convolution_bitcast_fusion
  93.0 0.8 copy.28
  93.7 4.9 %all-to-all-start.1 = ((f32[2,2,32,256]{3,0,1,2:T(2,128)}), f32[2,2,32,256]{3,0,1,2:T(2,128)S(1)}, u32[]{:S(2)}, u32[]{:S(2)}) async-start(f32[2,2,32,256]{3,0,1,2:T(2,128)} %copy.28), calls=%async_computation.1 | async-start | bytes 262144 | tf_op jit(solution)/shard_map/all_to_all | solution.py:231
  98.6 2.0 %fusion.36 = (f32[2048,64]{0,1:T(8,128)S(1)}, f32[2048,64]{0,1:T(8,128)S(1)}) fusion(s32[2048]{0:T(1024)S(1)} %get-tuple-element.12), kind=kLoop, calls=%fused_computation.42 | loop fusion | flops 1835008 | bytes 1056768 | tf_op jit(solution)/shard_map/cos | solution.py:51
  100.6 0.1 fusion.64
  100.8 0.1 copy.30
  100.9 0.2 fusion.63
  101.0 0.1 copy.31
  101.1 4.3 %all-to-all-done.1 = f32[2,2,32,256]{3,0,1,2:T(2,128)S(1)} async-done(((f32[2,2,32,256]{3,0,1,2:T(2,128)}), f32[2,2,32,256]{3,0,1,2:T(2,128)S(1)}, u32[]{:S(2)}, u32[]{:S(2)}) %all-to-all-start.1) | async-done | bytes 131104 | tf_op jit(solution)/shard_map/all_to_all | solution.py:231
  105.3 0.1 copy.43
  105.4 0.1 all_to_all.20
  105.5 3.5 %fusion.4 = f32[64,2,4,64]{3,0,2,1:T(8,128)S(1)} fusion(f32[2048,64]{0,1:T(8,128)S(1)} %get-tuple-element.14, f32[2,4,2048]{2,1,0:T(4,128)S(1)} %get-tuple-element.8, f32[2048,64]{0,1:T(8,128)S(1)} %get-tuple-element.13, f32[2,4,2048]{2,1,0:T(4,128)S(1)} %get-tuple-element.7, s32[2048]{0:T(1024)S(1)} %get-tuple-element.11), kind=kOutput, calls=%fused_computation.4 | convolution fusion | flops 808583168 | bytes 1318912 | tf_op jit(solution)/shard_map/tpcj,cv->tpvj/dot_general | solution.py:58
  109.0 3.5 %fusion = f32[64,2,4,64]{3,0,2,1:T(8,128)S(1)} fusion(f32[2048,64]{0,1:T(8,128)S(1)} %get-tuple-element.14, f32[2,4,2048]{2,1,0:T(4,128)S(1)} %get-tuple-element.8, f32[2048,64]{0,1:T(8,128)S(1)} %get-tuple-element.13, f32[2,4,2048]{2,1,0:T(4,128)S(1)} %get-tuple-element.7, s32[2048]{0:T(1024)S(1)} %get-tuple-element.11), kind=kOutput, calls=%fused_computation | convolution fusion | flops 808583168 | bytes 1318912 | tf_op jit(solution)/shard_map/tpcj,cv->tpvj/dot_general | solution.py:59
  112.5 0.5 fusion.27
  113.0 0.5 fusion.16
  113.6 0.8 reshape.270
  (7 shorter events, 0.1 us)
Async XLA Ops:
  0.0 2.4 %copy-start = (f32[2,17,2048]{2,0,1:T(2,128)S(1)}, f32[2,17,2048]{2,0,1:T(2,128)}, u32[]{:S(2)}) copy-start(f32[2,17,2048]{2,0,1:T(2,128)} %param.8) | copy-start | bytes 835588
  7.4 79.8 %copy-start.1 = (s32[2048]{0:T(1024)S(1)}, s32[2048]{0:T(1024)}, u32[]{:S(2)}) copy-start(s32[2048]{0:T(1024)} %param.11) | copy-start | bytes 24580
  81.8 10.7 %all-to-all-start = ((f32[4,2,2,17,256]{4,1,2,3,0:T(2,128)}), f32[4,2,2,17,256]{4,1,2,3,0:T(2,128)S(1)}, u32[]{:S(2)}, u32[]{:S(2)}) async-start(f32[4,2,2,17,256]{4,1,2,3,0:T(2,128)} %copy.25), calls=%async_computation | async-start | bytes 557056 | tf_op jit(solution)/shard_map/all_to_all | solution.py:228
  93.7 11.6 %all-to-all-start.1 = ((f32[2,2,32,256]{3,0,1,2:T(2,128)}), f32[2,2,32,256]{3,0,1,2:T(2,128)S(1)}, u32[]{:S(2)}, u32[]{:S(2)}) async-start(f32[2,2,32,256]{3,0,1,2:T(2,128)} %copy.28), calls=%async_computation.1 | async-start | bytes 262144 | tf_op jit(solution)/shard_map/all_to_all | solution.py:231

commit v2 on v1

v2 whole, which is shorter than its diff:
```python
import functools
import math

import jax
import jax.numpy as jnp
import numpy as np
from jax import lax
from jax.experimental import pallas as pl
from jax.experimental.pallas import tpu as pltpu
from jax.sharding import PartitionSpec as P

NPSI = 32
LANES = 128
TILE = 256
BLOCK = 8192
F32 = jnp.float32
BF16 = jnp.bfloat16


def psi_matrix(blks, cycles, orders):
    samples = NPSI // blks
    p = np.arange(NPSI).reshape(blks, 1, 1, samples, 1, 1, 1)
    cycle = np.arange(cycles)
    part = np.arange(2)
    k = np.arange(orders).reshape(1, 1, 1, 1, 1, orders, 1)
    same = cycle.reshape(1, -1, 1, 1, 1, 1, 1) == cycle.reshape(1, 1, 1, 1, -1, 1, 1)
    out_part = part.reshape(1, 1, 2, 1, 1, 1, 1)
    in_part = part.reshape(1, 1, 1, 1, 1, 1, 2)
    angle = 2.0 * np.pi * (k * p % NPSI) / NPSI
    turned = np.where(in_part == out_part, np.cos(angle), (out_part - in_part) * np.sin(angle))
    matrix = np.where(same, turned, 0.0).astype(np.float32)
    return matrix.reshape(blks * cycles * 2 * samples, cycles * orders * 2)


def psi_kernel(matrix_ref, parts_ref, out_ref):
    total = parts_ref[0]
    for e in range(1, parts_ref.shape[0]):
        total = total + parts_ref[e]
    out_ref[...] = jnp.dot(
        matrix_ref[...], total, precision=lax.Precision.HIGHEST, preferred_element_type=F32
    )


def to_psi(parts, blks, cycles, orders):
    matrix = psi_matrix(blks, cycles, orders)
    rows, cols = matrix.shape[0], parts.shape[2]
    out = pl.pallas_call(
        psi_kernel,
        out_shape=jax.ShapeDtypeStruct((rows, cols), F32),
        compiler_params=pltpu.CompilerParams(vmem_limit_bytes=16 * 2**20),
        name="psi",
    )(jnp.asarray(matrix), parts)
    return out.reshape(blks, rows // blks, cols)


def halves(array):
    upper = lax.reduce_precision(array, exponent_bits=8, mantissa_bits=7)
    return upper.astype(BF16), (array - upper).astype(BF16)


def phi_tables(order_of_column, period):
    def waves(step, count):
        turns = jnp.arange(count, dtype=jnp.int32)[:, None] * step * order_of_column[None, :]
        angle = (turns % period).astype(F32) * (2.0 * math.pi / period)
        return jnp.cos(angle), jnp.sin(angle)

    fine_cos, fine_sin = waves(1, LANES)
    return waves(LANES, period // LANES) + halves(fine_cos) + halves(-fine_sin)


def phi_kernel(cycles, fields_ref, cos_ref, sin_ref, ch_ref, cl_ref, sh_ref, sl_ref, out_ref):
    blks, rows, cols = fields_ref.shape
    samples = rows // (2 * cycles)
    coarse = cos_ref.shape[0]

    def nt(left, right):
        return lax.dot_general(
            left, right, (((1,), (1,)), ((), ())), preferred_element_type=F32
        )

    def split(pieces):
        array = jnp.concatenate(pieces, axis=0)
        upper = array.astype(BF16)
        return upper, (array - upper.astype(F32)).astype(BF16)

    wide = None
    narrow = None
    for d in range(blks):
        where = slice(d * cols, (d + 1) * cols)
        cos, sin = cos_ref[:, where], sin_ref[:, where]
        left_re, left_im = [], []
        for t in range(cycles):
            for p in range(samples):
                at = t * 2 * samples + p
                re = fields_ref[d, at : at + 1, :]
                im = fields_ref[d, at + samples : at + samples + 1, :]
                left_re.append(re * cos - im * sin)
                left_im.append(re * sin + im * cos)
        for left, high_ref, low_ref in ((left_re, ch_ref, cl_ref), (left_im, sh_ref, sl_ref)):
            upper, lower = split(left)
            high, low = high_ref[:, where], low_ref[:, where]
            both = nt(upper, jnp.concatenate([high, low], axis=0))
            rest = nt(lower, high)
            wide = both if wide is None else wide + both
            narrow = rest if narrow is None else narrow + rest
    fine = high_ref.shape[0]
    result = wide[:, 0:fine] + (wide[:, fine:] + narrow)
    for t in range(cycles):
        for p in range(samples):
            for a in range(coarse):
                at = (t * samples + p) * coarse + a
                out_ref[t, p : p + 1, a * fine : (a + 1) * fine] = result[at : at + 1]


def to_phi(fields, tables, cycles):
    blks, rows, cols = fields.shape
    coarse, fine = tables[0].shape[0], tables[2].shape[0]
    samples = rows // (2 * cycles)
    return pl.pallas_call(
        functools.partial(phi_kernel, cycles),
        out_shape=jax.ShapeDtypeStruct((cycles, samples, coarse * fine), F32),
        compiler_params=pltpu.CompilerParams(vmem_limit_bytes=40 * 2**20),
        name="phi",
    )(fields, *tables)


def sums_kernel(shape, col_ref, ell_ref, beam_ref, *refs):
    (cycles, orders, cols, spans, block, tail, steps, shares) = shape
    streams = refs[:-6]
    out_ref, sum_ref, values_ref, table_ref, rows_ref, turn_ref = refs[-6:]
    step = pl.program_id(0)
    degrees = beam_ref.shape[2]
    full = orders // 16 * 16
    pair = 2 * full

    def lowest_degree():
        def fold(at, width, low):
            where = pl.ds(at, width)
            col = col_ref[where].reshape(1, width)
            ell = ell_ref[where].reshape(1, width).astype(F32)
            return jnp.minimum(low, jnp.min(jnp.where(col >= 0, ell, float(degrees))))

        low = float(degrees)
        low = lax.fori_loop(
            0, steps, lambda i, c: fold(pl.multiple_of(i * block, block), block, c), jnp.float32(low)
        )
        if tail:
            low = fold(steps * block, tail, low)
        return jnp.minimum(low.astype(jnp.int32), degrees - spans * TILE)

    @pl.when(step == 0)
    def _():
        sum_ref[...] = jnp.zeros_like(sum_ref)
        rows_ref[...] = jnp.zeros_like(rows_ref)
        base = lowest_degree()
        for k in range(orders):
            window = pltpu.roll(beam_ref[k], degrees - base, 1)
            for j in range(spans):
                for r in range(2):
                    row = j * pair + r * full + k
                    if k >= full:
                        row = spans * pair + (k - full) * 16 + r * 8 + j
                    rows_ref[row : row + 1, 0:TILE] = window[r : r + 1, j * TILE : (j + 1) * TILE]
        rows = rows_ref[:, 0:TILE]
        upper = rows.astype(BF16)
        table_ref[0] = upper
        table_ref[1] = (rows - upper.astype(F32)).astype(BF16)
        rows_ref[0:1, TILE:] = jnp.zeros((1, LANES), F32) + base.astype(F32)

    def one_hot(row, count):
        rows = lax.broadcasted_iota(jnp.int32, (count, row.shape[1]), 0).astype(F32).astype(BF16)
        match = row.astype(F32).astype(BF16) == rows
        return jnp.where(match, jnp.ones_like(rows), jnp.zeros_like(rows))

    def add_chunk(w_ref, sky_ref, at, width):
        where = pl.ds(at, width)
        base = rows_ref[0:1, TILE : TILE + 1].astype(jnp.int32)
        index = ell_ref[where].reshape(1, width) - base
        span = lax.shift_right_arithmetic(index, 8)
        hot_ell = one_hot(lax.bitwise_and(index, TILE - 1), TILE)
        picked = jnp.dot(table_ref[0], hot_ell, preferred_element_type=F32) + jnp.dot(
            table_ref[1], hot_ell, preferred_element_type=F32
        )
        beam_re = picked[0:full]
        beam_im = picked[full:pair]
        for j in range(1, spans):
            here = span == j
            beam_re = jnp.where(here, picked[j * pair : j * pair + full], beam_re)
            beam_im = jnp.where(here, picked[j * pair + full : (j + 1) * pair], beam_im)
        sky_re = sky_ref[0:1, :]
        sky_im = sky_ref[1:2, :]
        coef_re = sky_re * beam_re - sky_im * beam_im
        coef_im = sky_re * beam_im + sky_im * beam_re
        rows8 = lax.broadcasted_iota(jnp.int32, (8, width), 0) == span
        for k in range(orders):
            if k < full:
                row_re = coef_re[k : k + 1]
                row_im = coef_im[k : k + 1]
            else:
                top = spans * pair + (k - full) * 16
                last_re = jnp.sum(jnp.where(rows8, picked[top : top + 8], 0.0), axis=0, keepdims=True)
                last_im = jnp.sum(
                    jnp.where(rows8, picked[top + 8 : top + 16], 0.0), axis=0, keepdims=True
                )
                row_re = sky_re * last_re - sky_im * last_im
                row_im = sky_re * last_im + sky_im * last_re
            w = w_ref[k].astype(F32)
            both = jnp.concatenate([w * row_re, w * row_im], axis=0).astype(BF16)
            values_ref[k * 2 * cycles : (k + 1) * 2 * cycles, 0:width] = both
        hot_col = one_hot(col_ref[where].reshape(1, width), cols)
        sum_ref[...] += lax.dot_general(
            values_ref[:, 0:width],
            hot_col,
            (((1,), (1,)), ((), ())),
            preferred_element_type=F32,
        )

    add_chunk(streams[0], streams[1], pl.multiple_of(step * block, block), block)

    @pl.when(step == steps - 1)
    def _():
        if tail:
            add_chunk(streams[2], streams[3], steps * block, tail)
        share = cycles // shares
        for half in range(0, cols, LANES):
            size = min(cols - half, LANES)
            turn_ref[half // LANES, :, 0:size] = sum_ref[:, half : half + size]
        for t in range(cycles):
            top = t % share * 2 * orders
            for half in range(0, cols, LANES):
                size = min(cols - half, LANES)
                every = turn_ref[half // LANES, pl.ds(t, 2 * orders, stride=cycles), :]
                out_ref[t // share, top : top + 2 * orders, half : half + size] = every[:, 0:size]


def column_sums(wigner, sky_alm, beam, slot_col, slot_ell, cols, spans, shares):
    orders, cycles, slots = wigner.shape
    block = min(BLOCK, 2 ** (slots.bit_length() - 1))
    steps = slots // block
    tail = slots - steps * block
    rows = 2 * orders * cycles
    full = orders // 16 * 16
    table_rows = spans * 2 * full + 16 * (orders - full)
    whole = pl.BlockSpec(memory_space=pltpu.VMEM)

    def specs(width, at):
        return [
            pl.BlockSpec((orders, cycles, width), lambda i: (0, 0, at(i))),
            pl.BlockSpec((2, width), lambda i: (0, at(i))),
        ]

    in_specs = [whole, whole, whole] + specs(block, lambda i: i)
    operands = [slot_col, slot_ell, beam, wigner, sky_alm]
    if tail:
        at = slots // tail - 1
        in_specs += specs(tail, lambda i: at)
        operands += [wigner, sky_alm]
    out_shape = (shares, rows // shares, cols)
    return pl.pallas_call(
        functools.partial(sums_kernel, (cycles, orders, cols, spans, block, tail, steps, shares)),
        grid=(steps,),
        in_specs=in_specs,
        out_specs=pl.BlockSpec(out_shape, lambda i: (0, 0, 0)),
        scratch_shapes=[
            pltpu.VMEM((rows, cols), F32),
            pltpu.VMEM((rows, block), BF16),
            pltpu.VMEM((2, table_rows, TILE), BF16),
            pltpu.VMEM((table_rows, TILE + LANES), F32),
            pltpu.VMEM((-(-cols // LANES), rows, LANES), F32),
        ],
        out_shape=jax.ShapeDtypeStruct(out_shape, F32),
        compiler_params=pltpu.CompilerParams(
            dimension_semantics=("arbitrary",), vmem_limit_bytes=60 * 2**20
        ),
        name="column_sums",
    )(*operands)


def degree_width(degrees, ell_count, blk_count, cols):
    live = degrees * (degrees + 1) // 2 // (ell_count * blk_count)
    width = degrees - (ell_count - 1) * live // cols
    return min(degrees, -(-width // TILE) * TILE)


def on_device(wigner, sky_alm, beam_blm, slot_col, slot_ell, order_of_column):
    cycle_total = wigner.shape[0]
    order_count = wigner.shape[1]
    slot_count = wigner.shape[2]
    ell_count = lax.axis_size("ell")
    blk_count = lax.axis_size("blk")
    col_count = order_of_column.shape[0] // blk_count
    cycle_share = cycle_total // ell_count
    degree_count = beam_blm.shape[2]
    width = degree_width(degree_count, ell_count, blk_count, col_count)
    spans = width // TILE
    parts = column_sums(
        jnp.transpose(wigner, (1, 0, 2)),
        sky_alm,
        jnp.transpose(beam_blm, (1, 0, 2)),
        slot_col,
        slot_ell,
        col_count,
        spans,
        ell_count,
    )
    tables = phi_tables(order_of_column, 2 * degree_count)
    parts = lax.all_to_all(parts, "ell", split_axis=0, concat_axis=0, tiled=True)
    fields = to_psi(parts, blk_count, cycle_share, order_count)
    fields = lax.all_to_all(fields, "blk", split_axis=0, concat_axis=0, tiled=True)
    return to_phi(fields, tables, cycle_share)


def solution(mesh):
    return jax.shard_map(
        on_device,
        mesh=mesh,
        in_specs=(
            P(None, None, ("ell", "blk")),
            P(None, ("ell", "blk")),
            P(),
            P(("ell", "blk")),
            P(("ell", "blk")),
            P(),
        ),
        out_specs=P("ell", "blk", None),
        check_vma=False,
    )
```

time: 115 us -> 57.2 us (0.50)
  Pallas kernels: 72.5 us -> 34.4 us
  matrix products: 8.35 us -> 0 us
  local copies, waits for them, and re-layouts: 7.99 us -> 0.01 us
  waiting for transfers between devices: 9.58 us -> 6.7 us
    pallas_call x1, Pallas kernels: 72.5 us -> 31.6 us  [column_sums(): pl.pallas_call(functools.partial(sums_kernel, (cycles, orders, cols, span...]
    dot_general x5 -> x0, matrix products: 8.35 us -> none  [the longest x1 3.48 us: to_phi(): jnp.einsum('tpcj,cv->tpvj', weighted_im, select, precision=highest)]
    reshape x6 -> x0, local copies, waits for them, and re-layouts: 6.55 us -> none  [the longest x1 1.84 us: on_device(): slot_ell.reshape(1, slot_count)]
    convert_element_type x1, other arithmetic: 0.02 us -> 4.56 us  [halves(): return (upper.astype(BF16), (array - upper).astype(BF16))]
    all_to_all x1, waiting for transfers between devices: 5.33 us -> 1.05 us  [on_device(): lax.all_to_all(parts, 'ell', split_axis=0, concat_axis=0, tiled=True)]
    pallas_call x0 -> x2, Pallas kernels: none -> 2.86 us  [the longest x1 1.95 us: to_phi(): pl.pallas_call(functools.partial(phi_kernel, cycles), out_shape=jax.Shape...]
    cos x2 -> x0, other arithmetic: 2.19 us -> none  [the longest x1 2.04 us: to_phi(): cos_first = jnp.cos(angle)]
    reduce_min x1 -> x0, other arithmetic: 1.78 us -> none  [on_device(): lowest = jnp.min(jnp.where(slot_col >= 0, slot_ell, degree_count))]
  transfers between devices with their start and end apart: 2 -> 2, of which waited for: 2 -> 2; matrix products, arithmetic and copies ran while one was open for 2% -> 10% of each run, Pallas kernels for 0% -> 0%
where the time goes in v2:
time: 57.2 us; the launch traced here: 56.9 us
  Pallas kernels  34.4 us (60%)
  starting transfers between devices  10.1 us (18%)
  waiting for transfers between devices  6.7 us (12%)
  other arithmetic  5.66 us (10%)
    pallas_call x1, Pallas kernels, column_sums(): pl.pallas_call(functools.partial(sums_kernel, (cycles, orders, cols, span...  31.6 us
    all_to_all x1, waiting for transfers between devices, on_device(): lax.all_to_all(fields, 'blk', split_axis=0, concat_axis=0, tiled=True)  5.65 us
    all_to_all x1, starting transfers between devices, on_device(): lax.all_to_all(parts, 'ell', split_axis=0, concat_axis=0, tiled=True)  5.19 us
    all_to_all x1, starting transfers between devices, on_device(): lax.all_to_all(fields, 'blk', split_axis=0, concat_axis=0, tiled=True)  4.87 us
    convert_element_type x1, other arithmetic, halves(): return (upper.astype(BF16), (array - upper).astype(BF16))  4.56 us
    pallas_call x1, Pallas kernels, to_phi(): pl.pallas_call(functools.partial(phi_kernel, cycles), out_shape=jax.Shape...  1.95 us
  transfers between devices with their start and end apart: 2, of which 2 were waited for; matrix products, arithmetic and copies ran while one was open for 10% of the time, Pallas kernels for 0%

profile of v2, /device:TPU:0, one launch (start us, length us, event | category | flops | bytes accessed | tf_op | source)
XLA Modules:
  0.0 56.9 jit_solution(9897009832768176345)
XLA Ops:
  0.0 0.0 copy-start.1
  0.0 0.0 copy-start
  0.0 31.6 %column_sums.1 = f32[4,68,256]{2,1,0:T(8,128)} custom-call(s32[65664]{0:T(1024)} %col_ref.1, s32[65664]{0:T(1024)} %ell_ref.1, f32[17,2,2048]{2,1,0:T(2,128)} %bitcast.5, bf16[17,8,65664]{2,1,0:T(8,128)(2,1)} %bitcast.3, f32[2,65664]{1,0:T(2,128)} %refs_3_.1, bf16[17,8,65664]{2,1,0:T(8,128)(2,1)} %bitcast.4, f32[2,65664]{1,0:T(2,128)} %refs_3_.1), custom_call_target="tpu_custom_call" | custom-call | tf_op jit(solution)/shard_map/column_sums/pallas_call | solution.py:259
  31.6 5.2 %all-to-all-start = ((f32[4,68,256]{2,1,0:T(8,128)}), f32[4,68,256]{2,1,0:T(8,128)S(1)}, u32[]{:S(2)}, u32[]{:S(2)}) async-start(f32[4,68,256]{2,1,0:T(8,128)} %column_sums.1), calls=%async_computation | async-start | bytes 589824 | tf_op jit(solution)/shard_map/all_to_all | solution.py:307
  36.8 0.0 copy-done.1
  36.8 4.6 %fusion.1 = (bf16[128,2048]{1,0:T(8,128)(2,1)S(1)}, bf16[128,2048]{1,0:T(8,128)(2,1)S(1)}, bf16[128,2048]{1,0:T(8,128)(2,1)S(1)}, bf16[128,2048]{1,0:T(8,128)(2,1)S(1)}) fusion(s32[2048]{0:T(1024)S(1)} %copy-done.1), kind=kLoop, calls=%fused_computation.8 | loop fusion | flops 6029312 | bytes 2105344 | tf_op jit(solution)/shard_map/convert_element_type | solution.py:58
  41.4 1.0 %all-to-all-done.parts_ref = f32[4,68,256]{2,1,0:T(8,128)S(1)} async-done(((f32[4,68,256]{2,1,0:T(8,128)}), f32[4,68,256]{2,1,0:T(8,128)S(1)}, u32[]{:S(2)}, u32[]{:S(2)}) %all-to-all-start) | async-done | bytes 278560 | tf_op jit(solution)/shard_map/all_to_all | solution.py:307
  42.4 0.0 copy-done
  42.4 0.9 %psi.1 = f32[128,256]{1,0:T(8,128)} custom-call(f32[128,68]{1,0:T(8,128)S(1)} %copy-done, f32[4,68,256]{2,1,0:T(8,128)S(1)} %all-to-all-done.parts_ref), custom_call_target="tpu_custom_call" | custom-call | tf_op jit(solution)/shard_map/psi/pallas_call | solution.py:47
  43.3 4.9 %all-to-all-start.1 = ((f32[8,16,256]{2,1,0:T(8,128)}), f32[8,16,256]{2,1,0:T(8,128)S(1)}, u32[]{:S(2)}, u32[]{:S(2)}) async-start(f32[8,16,256]{2,1,0:T(8,128)} %bitcast.2), calls=%async_computation.1 | async-start | bytes 262144 | tf_op jit(solution)/shard_map/all_to_all | solution.py:309
  48.2 1.1 %fusion.12 = (f32[32,2048]{1,0:T(8,128)S(1)}, f32[32,2048]{1,0:T(8,128)S(1)}) fusion(s32[2048]{0:T(1024)S(1)} %copy-done.1, s32[32]{0:T(128)S(1)} %iota_multiply_fusion), kind=kLoop, calls=%fused_computation.25 | loop fusion | flops 917504 | bytes 532608 | tf_op jit(solution)/shard_map/sin | solution.py:65
  49.3 5.6 %all-to-all-done.1.fields_ref = f32[8,16,256]{2,1,0:T(8,128)S(1)} async-done(((f32[8,16,256]{2,1,0:T(8,128)}), f32[8,16,256]{2,1,0:T(8,128)S(1)}, u32[]{:S(2)}, u32[]{:S(2)}) %all-to-all-start.1) | async-done | bytes 131104 | tf_op jit(solution)/shard_map/all_to_all | solution.py:309
  54.9 1.9 %phi.1 = f32[2,4,4096]{2,1,0:T(4,128)} custom-call(f32[8,16,256]{2,1,0:T(8,128)S(1)} %all-to-all-done.1.fields_ref, f32[32,2048]{1,0:T(8,128)S(1)} %get-tuple-element.6.cos_ref, f32[32,2048]{1,0:T(8,128)S(1)} %get-tuple-element.5.sin_ref, bf16[128,2048]{1,0:T(8,128)(2,1)S(1)} %get-tuple-element.10.ch_ref, bf16[128,2048]{1,0:T(8,128)(2,1)S(1)} %get-tuple-element.8.cl_ref, ...), custom_call_target="tpu_custom_call" | custom-call | tf_op jit(solution)/shard_map/phi/pallas_call | solution.py:119
  (1 shorter events, 0.0 us)
Async XLA Ops:
  0.0 36.8 %copy-start.1 = (s32[2048]{0:T(1024)S(1)}, s32[2048]{0:T(1024)}, u32[]{:S(2)}) copy-start(s32[2048]{0:T(1024)} %param.12) | copy-start | bytes 24580
  0.0 42.4 %copy-start = (f32[128,68]{1,0:T(8,128)S(1)}, f32[128,68]{1,0:T(8,128)}, u32[]{:S(2)}) copy-start(f32[128,68]{1,0:T(8,128)} %constant.30.clone.matrix_ref) | copy-start | bytes 104452
  31.6 10.8 %all-to-all-start = ((f32[4,68,256]{2,1,0:T(8,128)}), f32[4,68,256]{2,1,0:T(8,128)S(1)}, u32[]{:S(2)}, u32[]{:S(2)}) async-start(f32[4,68,256]{2,1,0:T(8,128)} %column_sums.1), calls=%async_computation | async-start | bytes 589824 | tf_op jit(solution)/shard_map/all_to_all | solution.py:307
  43.3 11.6 %all-to-all-start.1 = ((f32[8,16,256]{2,1,0:T(8,128)}), f32[8,16,256]{2,1,0:T(8,128)S(1)}, u32[]{:S(2)}, u32[]{:S(2)}) async-start(f32[8,16,256]{2,1,0:T(8,128)} %bitcast.2), calls=%async_computation.1 | async-start | bytes 262144 | tf_op jit(solution)/shard_map/all_to_all | solution.py:309

commit v3 on v2

--- a/solution.py
+++ b/solution.py
@@ -12,7 +12,8 @@
 NPSI = 32
 LANES = 128
 TILE = 256
-BLOCK = 8192
+BLOCK = 16384
+PIECE = 1024
 F32 = jnp.float32
 BF16 = jnp.bfloat16
 
@@ -22,34 +23,34 @@
     p = np.arange(NPSI).reshape(blks, 1, 1, samples, 1, 1, 1)
     cycle = np.arange(cycles)
     part = np.arange(2)
-    k = np.arange(orders).reshape(1, 1, 1, 1, 1, orders, 1)
+    k = np.arange(orders).reshape(1, 1, 1, 1, 1, 1, orders)
     same = cycle.reshape(1, -1, 1, 1, 1, 1, 1) == cycle.reshape(1, 1, 1, 1, -1, 1, 1)
     out_part = part.reshape(1, 1, 2, 1, 1, 1, 1)
-    in_part = part.reshape(1, 1, 1, 1, 1, 1, 2)
+    in_part = part.reshape(1, 1, 1, 1, 1, 2, 1)
     angle = 2.0 * np.pi * (k * p % NPSI) / NPSI
     turned = np.where(in_part == out_part, np.cos(angle), (out_part - in_part) * np.sin(angle))
     matrix = np.where(same, turned, 0.0).astype(np.float32)
     return matrix.reshape(blks * cycles * 2 * samples, cycles * orders * 2)
 
 
-def psi_kernel(matrix_ref, parts_ref, out_ref):
-    total = parts_ref[0]
-    for e in range(1, parts_ref.shape[0]):
-        total = total + parts_ref[e]
-    out_ref[...] = jnp.dot(
+def psi_kernel(matrix_ref, *refs):
+    total = refs[0][...]
+    for part_ref in refs[1:-1]:
+        total = total + part_ref[...]
+    refs[-1][...] = jnp.dot(
         matrix_ref[...], total, precision=lax.Precision.HIGHEST, preferred_element_type=F32
     )
 
 
 def to_psi(parts, blks, cycles, orders):
     matrix = psi_matrix(blks, cycles, orders)
-    rows, cols = matrix.shape[0], parts.shape[2]
+    rows, cols = matrix.shape[0], parts[0].shape[1]
     out = pl.pallas_call(
         psi_kernel,
         out_shape=jax.ShapeDtypeStruct((rows, cols), F32),
         compiler_params=pltpu.CompilerParams(vmem_limit_bytes=16 * 2**20),
         name="psi",
-    )(jnp.asarray(matrix), parts)
+    )(jnp.asarray(matrix), *parts)
     return out.reshape(blks, rows // blks, cols)
 
 
@@ -124,10 +125,11 @@
     )(fields, *tables)
 
 
-def sums_kernel(shape, col_ref, ell_ref, beam_ref, *refs):
+def sums_kernel(shape, me_ref, col_ref, ell_ref, beam_ref, *refs):
     (cycles, orders, cols, spans, block, tail, steps, shares) = shape
-    streams = refs[:-6]
-    out_ref, sum_ref, values_ref, table_ref, rows_ref, turn_ref = refs[-6:]
+    streams = refs[: -6 - shares]
+    out_refs = refs[-6 - shares : -6]
+    sum_ref, values_ref, table_ref, rows_ref, turn_ref, coef_ref = refs[-6:]
     step = pl.program_id(0)
     degrees = beam_ref.shape[2]
     full = orders // 16 * 16
@@ -159,7 +161,7 @@
                 for r in range(2):
                     row = j * pair + r * full + k
                     if k >= full:
-                        row = spans * pair + (k - full) * 16 + r * 8 + j
+                        row = spans * pair + (k - full) * 16 + 2 * j + r
                     rows_ref[row : row + 1, 0:TILE] = window[r : r + 1, j * TILE : (j + 1) * TILE]
         rows = rows_ref[:, 0:TILE]
         upper = rows.astype(BF16)
@@ -172,10 +174,8 @@
         match = row.astype(F32).astype(BF16) == rows
         return jnp.where(match, jnp.ones_like(rows), jnp.zeros_like(rows))
 
-    def add_chunk(w_ref, sky_ref, at, width):
-        where = pl.ds(at, width)
-        base = rows_ref[0:1, TILE : TILE + 1].astype(jnp.int32)
-        index = ell_ref[where].reshape(1, width) - base
+    def pick(sky_ref, first, at, width):
+        index = ell_ref[pl.ds(at, width)].reshape(1, width) - base
         span = lax.shift_right_arithmetic(index, 8)
         hot_ell = one_hot(lax.bitwise_and(index, TILE - 1), TILE)
         picked = jnp.dot(table_ref[0], hot_ell, preferred_element_type=F32) + jnp.dot(
@@ -187,27 +187,55 @@
             here = span == j
             beam_re = jnp.where(here, picked[j * pair : j * pair + full], beam_re)
             beam_im = jnp.where(here, picked[j * pair + full : (j + 1) * pair], beam_im)
-        sky_re = sky_ref[0:1, :]
-        sky_im = sky_ref[1:2, :]
-        coef_re = sky_re * beam_re - sky_im * beam_im
-        coef_im = sky_re * beam_im + sky_im * beam_re
-        rows8 = lax.broadcasted_iota(jnp.int32, (8, width), 0) == span
-        for k in range(orders):
-            if k < full:
-                row_re = coef_re[k : k + 1]
-                row_im = coef_im[k : k + 1]
-            else:
-                top = spans * pair + (k - full) * 16
-                last_re = jnp.sum(jnp.where(rows8, picked[top : top + 8], 0.0), axis=0, keepdims=True)
-                last_im = jnp.sum(
-                    jnp.where(rows8, picked[top + 8 : top + 16], 0.0), axis=0, keepdims=True
-                )
-                row_re = sky_re * last_re - sky_im * last_im
-                row_im = sky_re * last_im + sky_im * last_re
-            w = w_ref[k].astype(F32)
-            both = jnp.concatenate([w * row_re, w * row_im], axis=0).astype(BF16)
-            values_ref[k * 2 * cycles : (k + 1) * 2 * cycles, 0:width] = both
-        hot_col = one_hot(col_ref[where].reshape(1, width), cols)
+        sky_re = sky_ref[0:1, first : first + width]
+        sky_im = sky_ref[1:2, first : first + width]
+        tiles = width // LANES
+        start = first // LANES
+
+        def keep(row, array):
+            for i in range(tiles):
+                coef_ref[start + i, row : row + array.shape[0], :] = array[
+                    :, i * LANES : (i + 1) * LANES
+                ]
+
+        keep(0, sky_re * beam_re - sky_im * beam_im)
+        keep(full, sky_re * beam_im + sky_im * beam_re)
+        rows8 = lax.broadcasted_iota(jnp.int32, (8, width), 0)
+        of_span = lax.shift_right_logical(rows8, 1)
+        odd = lax.bitwise_and(rows8, 1) == 1
+        signed = jnp.where(odd, sky_im, -sky_im)
+        for k in range(full, orders):
+            top = spans * pair + (k - full) * 16
+            both = jnp.where(of_span == span, picked[top : top + 8], 0.0)
+            if spans > 4:
+                both = jnp.where(of_span + 4 == span, picked[top + 8 : top + 16], both)
+            both = both + pltpu.roll(both, 4, 0)
+            both = both + pltpu.roll(both, 2, 0)
+            keep(pair + (k - full) * 8, both * sky_re + pltpu.roll(both, 1, 0) * signed)
+
+    def spread(w_ref, first, width):
+        for i in range(first // LANES, (first + width) // LANES):
+            lanes = slice(i * LANES, (i + 1) * LANES)
+            for k in range(orders):
+                re_row, im_row = k, full + k
+                if k >= full:
+                    re_row = pair + (k - full) * 8
+                    im_row = re_row + 1
+                row_re = coef_ref[i, pl.ds(re_row, 8, stride=0), :]
+                row_im = coef_ref[i, pl.ds(im_row, 8, stride=0), :]
+                w = w_ref[k, :, lanes].astype(F32)
+                for c in range(0, cycles, 8):
+                    part = w[c : c + 8]
+                    top = k * 2 * cycles + 2 * c
+                    both = jnp.concatenate([part * row_re, part * row_im], axis=0).astype(BF16)
+                    values_ref[top : top + 16, lanes] = both
+
+    def add_chunk(w_ref, sky_ref, at, width):
+        part = min(width, PIECE)
+        for first in range(0, width, part):
+            pick(sky_ref, first, at + first, part)
+            spread(w_ref, first, part)
+        hot_col = one_hot(col_ref[pl.ds(at, width)].reshape(1, width), cols)
         sum_ref[...] += lax.dot_general(
             values_ref[:, 0:width],
             hot_col,
@@ -215,6 +243,7 @@
             preferred_element_type=F32,
         )
 
+    base = rows_ref[0:1, TILE : TILE + 1].astype(jnp.int32)
     add_chunk(streams[0], streams[1], pl.multiple_of(step * block, block), block)
 
     @pl.when(step == steps - 1)
@@ -225,15 +254,20 @@
         for half in range(0, cols, LANES):
             size = min(cols - half, LANES)
             turn_ref[half // LANES, :, 0:size] = sum_ref[:, half : half + size]
-        for t in range(cycles):
-            top = t % share * 2 * orders
-            for half in range(0, cols, LANES):
-                size = min(cols - half, LANES)
-                every = turn_ref[half // LANES, pl.ds(t, 2 * orders, stride=cycles), :]
-                out_ref[t // share, top : top + 2 * orders, half : half + size] = every[:, 0:size]
-
-
-def column_sums(wigner, sky_alm, beam, slot_col, slot_ell, cols, spans, shares):
+        for d in range(shares):
+            for i in range(share):
+                t = lax.bitwise_xor(me_ref[0], d) * share + i
+                start = t // 8 * 16 + t % 8
+                for r in range(2):
+                    top = (2 * i + r) * orders
+                    rows = pl.ds(start + r * 8, orders, stride=2 * cycles)
+                    for lane in range(0, cols, LANES):
+                        size = min(cols - lane, LANES)
+                        every = turn_ref[lane // LANES, rows, :]
+                        out_refs[d][top : top + orders, lane : lane + size] = every[:, 0:size]
+
+
+def column_sums(me, wigner, sky_alm, beam, slot_col, slot_ell, cols, spans, shares):
     orders, cycles, slots = wigner.shape
     block = min(BLOCK, 2 ** (slots.bit_length() - 1))
     steps = slots // block
@@ -249,26 +283,27 @@
             pl.BlockSpec((2, width), lambda i: (0, at(i))),
         ]
 
-    in_specs = [whole, whole, whole] + specs(block, lambda i: i)
-    operands = [slot_col, slot_ell, beam, wigner, sky_alm]
+    in_specs = [pl.BlockSpec(memory_space=pltpu.SMEM), whole, whole, whole] + specs(block, lambda i: i)
+    operands = [me, slot_col, slot_ell, beam, wigner, sky_alm]
     if tail:
         at = slots // tail - 1
         in_specs += specs(tail, lambda i: at)
         operands += [wigner, sky_alm]
-    out_shape = (shares, rows // shares, cols)
+    out_shape = (rows // shares, cols)
     return pl.pallas_call(
         functools.partial(sums_kernel, (cycles, orders, cols, spans, block, tail, steps, shares)),
         grid=(steps,),
         in_specs=in_specs,
-        out_specs=pl.BlockSpec(out_shape, lambda i: (0, 0, 0)),
+        out_specs=[pl.BlockSpec(out_shape, lambda i: (0, 0))] * shares,
         scratch_shapes=[
             pltpu.VMEM((rows, cols), F32),
             pltpu.VMEM((rows, block), BF16),
             pltpu.VMEM((2, table_rows, TILE), BF16),
             pltpu.VMEM((table_rows, TILE + LANES), F32),
             pltpu.VMEM((-(-cols // LANES), rows, LANES), F32),
+            pltpu.VMEM((block // LANES, 2 * full + 8 * (orders - full), LANES), F32),
         ],
-        out_shape=jax.ShapeDtypeStruct(out_shape, F32),
+        out_shape=[jax.ShapeDtypeStruct(out_shape, F32)] * shares,
         compiler_params=pltpu.CompilerParams(
             dimension_semantics=("arbitrary",), vmem_limit_bytes=60 * 2**20
         ),
@@ -294,6 +329,7 @@
     width = degree_width(degree_count, ell_count, blk_count, col_count)
     spans = width // TILE
     parts = column_sums(
+        lax.axis_index("ell").reshape(1),
         jnp.transpose(wigner, (1, 0, 2)),
         sky_alm,
         jnp.transpose(beam_blm, (1, 0, 2)),
@@ -304,7 +340,10 @@
         ell_count,
     )
     tables = phi_tables(order_of_column, 2 * degree_count)
-    parts = lax.all_to_all(parts, "ell", split_axis=0, concat_axis=0, tiled=True)
+    parts = [
+        part if d == 0 else lax.ppermute(part, "ell", [(i, i ^ d) for i in range(ell_count)])
+        for d, part in enumerate(parts)
+    ]
     fields = to_psi(parts, blk_count, cycle_share, order_count)
     fields = lax.all_to_all(fields, "blk", split_axis=0, concat_axis=0, tiled=True)
     return to_phi(fields, tables, cycle_share)

time: 57.2 us -> 55.5 us (0.970)
  Pallas kernels: 34.4 us -> 32.7 us
  local copies, waits for them, and re-layouts: 0.01 us -> 0.89 us
  starting transfers between devices: 10.1 us -> 9.42 us
    all_to_all x1 -> x0, starting transfers between devices: 5.19 us -> none  [on_device(): lax.all_to_all(parts, 'ell', split_axis=0, concat_axis=0, tiled=True)]
    ppermute x0 -> x3, starting transfers between devices: none -> 4.54 us  [on_device(): lax.ppermute(part, 'ell', [(i, i ^ d) for i in range(ell_count)])]
    pallas_call x1, Pallas kernels: 31.6 us -> 29.8 us  [column_sums(): pl.pallas_call(functools.partial(sums_kernel, (cycles, orders, cols, span...]
    all_to_all x1 -> x0, waiting for transfers between devices: 1.05 us -> none  [on_device(): lax.all_to_all(parts, 'ell', split_axis=0, concat_axis=0, tiled=True)]
    unnamed x4 -> x6, local copies, waits for them, and re-layouts: 0.01 us -> 0.89 us
    ppermute x0 -> x3, waiting for transfers between devices: none -> 0.85 us  [on_device(): lax.ppermute(part, 'ell', [(i, i ^ d) for i in range(ell_count)])]
  transfers between devices with their start and end apart: 2 -> 4, of which waited for: 2 -> 2; matrix products, arithmetic and copies ran while one was open for 10% -> 10% of each run, Pallas kernels for 0% -> 0%
where the time goes in v3:
time: 55.5 us; the launch traced here: 55.2 us
  Pallas kernels  32.7 us (59%)
  starting transfers between devices  9.42 us (17%)
  waiting for transfers between devices  6.5 us (12%)
  other arithmetic  5.66 us (10%)
  local copies, waits for them, and re-layouts  0.89 us (2%)
    pallas_call x1, Pallas kernels, column_sums(): pl.pallas_call(functools.partial(sums_kernel, (cycles, orders, cols, span...  29.8 us
    all_to_all x1, waiting for transfers between devices, on_device(): lax.all_to_all(fields, 'blk', split_axis=0, concat_axis=0, tiled=True)  5.65 us
    all_to_all x1, starting transfers between devices, on_device(): lax.all_to_all(fields, 'blk', split_axis=0, concat_axis=0, tiled=True)  4.88 us
    convert_element_type x1, other arithmetic, halves(): return (upper.astype(BF16), (array - upper).astype(BF16))  4.56 us
    ppermute x3, starting transfers between devices, on_device(): lax.ppermute(part, 'ell', [(i, i ^ d) for i in range(ell_count)])  4.54 us
    pallas_call x1, Pallas kernels, to_phi(): pl.pallas_call(functools.partial(phi_kernel, cycles), out_shape=jax.Shape...  1.95 us
  transfers between devices with their start and end apart: 4, of which 2 were waited for; matrix products, arithmetic and copies ran while one was open for 10% of the time, Pallas kernels for 0%

profile of v3, /device:TPU:0, one launch (start us, length us, event | category | flops | bytes accessed | tf_op | source)
XLA Modules:
  0.0 55.2 jit_solution(8565227489105545063)
XLA Ops:
  0.0 0.0 copy-start.2
  0.0 0.0 copy-start.1
  0.0 29.8 %column_sums.1 = (f32[68,256]{1,0:T(8,128)}, f32[68,256]{1,0:T(8,128)}, f32[68,256]{1,0:T(8,128)}, f32[68,256]{1,0:T(8,128)}) custom-call(s32[1]{0:T(128)} %bitcast.me_ref, s32[65664]{0:T(1024)} %col_ref.1, s32[65664]{0:T(1024)} %ell_ref.1, f32[17,2,2048]{2,1,0:T(2,128)} %bitcast.6, bf16[17,8,65664]{2,1,0:T(8,128)(2,1)} %bitcast.4, f32[2,65664]{1,0:T(2,128)} %refs_3_.1, ...), custom_call_target="tpu_custom_call" | custom-call | tf_op jit(solution)/shard_map/column_sums/pallas_call | solution.py:293
  29.8 3.0 %collective-permute-start = (f32[68,256]{1,0:T(8,128)}, f32[68,256]{1,0:T(8,128)S(1)}, u32[]{:S(2)}, u32[]{:S(2)}) collective-permute-start(f32[68,256]{1,0:T(8,128)} %get-tuple-element.10), channel_id=1, source_target_pairs={{0,8},{8,0},{16,24},{24,16},{1,9},{9,1},{17,25},{25,17},{2,10},{10... | collective-permute-start | bytes 208904 | tf_op jit(solution)/shard_map/ppermute | solution.py:344
  32.8 1.5 %collective-permute-start.1 = (f32[68,256]{1,0:T(8,128)}, f32[68,256]{1,0:T(8,128)S(1)}, u32[]{:S(2)}, u32[]{:S(2)}) collective-permute-start(f32[68,256]{1,0:T(8,128)} %get-tuple-element.11), channel_id=1, source_target_pairs={{0,16},{8,24},{16,0},{24,8},{1,17},{9,25},{17,1},{25,9},{2,18},{10... | collective-permute-start | bytes 208904 | tf_op jit(solution)/shard_map/ppermute | solution.py:344
  34.4 0.0 collective-permute-start.2
  34.4 0.0 copy-done.2
  34.4 4.6 %fusion.1 = (bf16[128,2048]{1,0:T(8,128)(2,1)S(1)}, bf16[128,2048]{1,0:T(8,128)(2,1)S(1)}, bf16[128,2048]{1,0:T(8,128)(2,1)S(1)}, bf16[128,2048]{1,0:T(8,128)(2,1)S(1)}) fusion(s32[2048]{0:T(1024)S(1)} %copy-done.2), kind=kLoop, calls=%fused_computation.8 | loop fusion | flops 6029312 | bytes 2105344 | tf_op jit(solution)/shard_map/convert_element_type | solution.py:59
  39.0 0.0 collective-permute-done.refs_1_
  39.0 0.0 collective-permute-done.1.refs_2_
  39.0 0.8 %collective-permute-done.2.refs_3_ = f32[68,256]{1,0:T(8,128)S(1)} collective-permute-done((f32[68,256]{1,0:T(8,128)}, f32[68,256]{1,0:T(8,128)S(1)}, u32[]{:S(2)}, u32[]{:S(2)}) %collective-permute-start.2) | collective-permute-done | bytes 69664 | tf_op jit(solution)/shard_map/ppermute | solution.py:344
  39.8 0.0 copy-done.1
  39.8 0.0 copy-start
  39.8 0.9 %copy-done = f32[68,256]{1,0:T(8,128)S(1)} copy-done((f32[68,256]{1,0:T(8,128)S(1)}, f32[68,256]{1,0:T(8,128)}, u32[]{:S(2)}) %copy-start) | copy-done | bytes 69656
  40.7 0.9 %psi.1 = f32[128,256]{1,0:T(8,128)} custom-call(f32[128,68]{1,0:T(8,128)S(1)} %copy-done.1, f32[68,256]{1,0:T(8,128)S(1)} %copy-done, f32[68,256]{1,0:T(8,128)S(1)} %collective-permute-done.refs_1_, f32[68,256]{1,0:T(8,128)S(1)} %collective-permute-done.1.refs_2_, f32[68,256]{1,0:T(8,128)S(1)} %collective-permute-done.2.refs_3_), custom_call_target="tpu_custom_call" | custom-call | tf_op jit(solution)/shard_map/psi/pallas_call | solution.py:48
  41.6 4.9 %all-to-all-start = ((f32[8,16,256]{2,1,0:T(8,128)}), f32[8,16,256]{2,1,0:T(8,128)S(1)}, u32[]{:S(2)}, u32[]{:S(2)}) async-start(f32[8,16,256]{2,1,0:T(8,128)} %bitcast.3), calls=%async_computation | async-start | bytes 262144 | tf_op jit(solution)/shard_map/all_to_all | solution.py:348
  46.5 1.1 %fusion.12 = (f32[32,2048]{1,0:T(8,128)S(1)}, f32[32,2048]{1,0:T(8,128)S(1)}) fusion(s32[2048]{0:T(1024)S(1)} %copy-done.2, s32[32]{0:T(128)S(1)} %iota_multiply_fusion), kind=kLoop, calls=%fused_computation.25 | loop fusion | flops 917504 | bytes 532608 | tf_op jit(solution)/shard_map/sin | solution.py:66
  47.6 5.6 %all-to-all-done.fields_ref = f32[8,16,256]{2,1,0:T(8,128)S(1)} async-done(((f32[8,16,256]{2,1,0:T(8,128)}), f32[8,16,256]{2,1,0:T(8,128)S(1)}, u32[]{:S(2)}, u32[]{:S(2)}) %all-to-all-start) | async-done | bytes 131104 | tf_op jit(solution)/shard_map/all_to_all | solution.py:348
  53.3 2.0 %phi.1 = f32[2,4,4096]{2,1,0:T(4,128)} custom-call(f32[8,16,256]{2,1,0:T(8,128)S(1)} %all-to-all-done.fields_ref, f32[32,2048]{1,0:T(8,128)S(1)} %get-tuple-element.14.cos_ref, f32[32,2048]{1,0:T(8,128)S(1)} %get-tuple-element.13.sin_ref, bf16[128,2048]{1,0:T(8,128)(2,1)S(1)} %get-tuple-element.18.ch_ref, bf16[128,2048]{1,0:T(8,128)(2,1)S(1)} %get-tuple-element.16.cl_ref, ...), custom_call_target="tpu_custom_call" | custom-call | tf_op jit(solution)/shard_map/phi/pallas_call | solution.py:120
  (1 shorter events, 0.0 us)
Async XLA Ops:
  0.0 34.4 %copy-start.2 = (s32[2048]{0:T(1024)S(1)}, s32[2048]{0:T(1024)}, u32[]{:S(2)}) copy-start(s32[2048]{0:T(1024)} %param.12) | copy-start | bytes 24580
  0.0 39.8 %copy-start.1 = (f32[128,68]{1,0:T(8,128)S(1)}, f32[128,68]{1,0:T(8,128)}, u32[]{:S(2)}) copy-start(f32[128,68]{1,0:T(8,128)} %constant.35.clone.matrix_ref) | copy-start | bytes 104452
  29.8 9.1 %collective-permute-start = (f32[68,256]{1,0:T(8,128)}, f32[68,256]{1,0:T(8,128)S(1)}, u32[]{:S(2)}, u32[]{:S(2)}) collective-permute-start(f32[68,256]{1,0:T(8,128)} %get-tuple-element.10), channel_id=1, source_target_pairs={{0,8},{8,0},{16,24},{24,16},{1,9},{9,1},{17,25},{25,17},{2,10},{10... | collective-permute-start | bytes 208904 | tf_op jit(solution)/shard_map/ppermute | solution.py:344
  32.8 6.1 %collective-permute-start.1 = (f32[68,256]{1,0:T(8,128)}, f32[68,256]{1,0:T(8,128)S(1)}, u32[]{:S(2)}, u32[]{:S(2)}) collective-permute-start(f32[68,256]{1,0:T(8,128)} %get-tuple-element.11), channel_id=1, source_target_pairs={{0,16},{8,24},{16,0},{24,8},{1,17},{9,25},{17,1},{25,9},{2,18},{10... | collective-permute-start | bytes 208904 | tf_op jit(solution)/shard_map/ppermute | solution.py:344
  34.4 5.5 %collective-permute-start.2 = (f32[68,256]{1,0:T(8,128)}, f32[68,256]{1,0:T(8,128)S(1)}, u32[]{:S(2)}, u32[]{:S(2)}) collective-permute-start(f32[68,256]{1,0:T(8,128)} %get-tuple-element.12), channel_id=1, source_target_pairs={{0,24},{8,16},{16,8},{24,0},{1,25},{9,17},{17,9},{25,1},{2,26},{10... | collective-permute-start | bytes 208904 | tf_op jit(solution)/shard_map/ppermute | solution.py:344
  39.8 0.9 %copy-start = (f32[68,256]{1,0:T(8,128)S(1)}, f32[68,256]{1,0:T(8,128)}, u32[]{:S(2)}) copy-start(f32[68,256]{1,0:T(8,128)} %get-tuple-element.9.refs_0_) | copy-start | bytes 208900
  41.6 11.6 %all-to-all-start = ((f32[8,16,256]{2,1,0:T(8,128)}), f32[8,16,256]{2,1,0:T(8,128)S(1)}, u32[]{:S(2)}, u32[]{:S(2)}) async-start(f32[8,16,256]{2,1,0:T(8,128)} %bitcast.3), calls=%async_computation | async-start | bytes 262144 | tf_op jit(solution)/shard_map/all_to_all | solution.py:348

commit v4 on v3

--- a/solution.py
+++ b/solution.py
@@ -125,15 +125,48 @@
     )(fields, *tables)
 
 
-def sums_kernel(shape, me_ref, col_ref, ell_ref, beam_ref, *refs):
+def sums_kernel(shape, me_ref, *refs):
     (cycles, orders, cols, spans, block, tail, steps, shares) = shape
-    streams = refs[: -6 - shares]
-    out_refs = refs[-6 - shares : -6]
-    sum_ref, values_ref, table_ref, rows_ref, turn_ref, coef_ref = refs[-6:]
-    step = pl.program_id(0)
+    sources, wigner_ref, out_refs = refs[:4], refs[4], refs[5 : 5 + shares]
+    (
+        sum_ref,
+        values_ref,
+        table_ref,
+        rows_ref,
+        turn_ref,
+        coef_ref,
+        held_ref,
+        last_ref,
+        col_ref,
+        ell_ref,
+        beam_ref,
+        sky_ref,
+        sems,
+    ) = refs[5 + shares :]
     degrees = beam_ref.shape[2]
     full = orders // 16 * 16
     pair = 2 * full
+
+    def arrival(i):
+        where = pl.ds(pl.multiple_of(i * block, block), block)
+        slot = lax.rem(i, 2)
+        return pltpu.make_async_copy(
+            wigner_ref.at[:, :, where], held_ref.at[slot], sems.at[slot]
+        )
+
+    def last_arrival():
+        where = pl.ds(steps * block, tail)
+        return pltpu.make_async_copy(wigner_ref.at[:, :, where], last_ref, sems.at[2])
+
+    small = [
+        pltpu.make_async_copy(source, target, sems.at[3 + i])
+        for i, (source, target) in enumerate(zip(sources, (col_ref, ell_ref, beam_ref, sky_ref)))
+    ]
+    for copy in small:
+        copy.start()
+    arrival(0).start()
+    if tail:
+        last_arrival().start()
 
     def lowest_degree():
         def fold(at, width, low):
@@ -150,31 +183,31 @@
             low = fold(steps * block, tail, low)
         return jnp.minimum(low.astype(jnp.int32), degrees - spans * TILE)
 
-    @pl.when(step == 0)
-    def _():
-        sum_ref[...] = jnp.zeros_like(sum_ref)
-        rows_ref[...] = jnp.zeros_like(rows_ref)
-        base = lowest_degree()
-        for k in range(orders):
-            window = pltpu.roll(beam_ref[k], degrees - base, 1)
-            for j in range(spans):
-                for r in range(2):
-                    row = j * pair + r * full + k
-                    if k >= full:
-                        row = spans * pair + (k - full) * 16 + 2 * j + r
-                    rows_ref[row : row + 1, 0:TILE] = window[r : r + 1, j * TILE : (j + 1) * TILE]
-        rows = rows_ref[:, 0:TILE]
-        upper = rows.astype(BF16)
-        table_ref[0] = upper
-        table_ref[1] = (rows - upper.astype(F32)).astype(BF16)
-        rows_ref[0:1, TILE:] = jnp.zeros((1, LANES), F32) + base.astype(F32)
+    sum_ref[...] = jnp.zeros_like(sum_ref)
+    rows_ref[...] = jnp.zeros_like(rows_ref)
+    for copy in small:
+        copy.wait()
+    base = lowest_degree()
+    for k in range(orders):
+        window = pltpu.roll(beam_ref[k], degrees - base, 1)
+        for j in range(spans):
+            for r in range(2):
+                row = j * pair + r * full + k
+                if k >= full:
+                    row = spans * pair + (k - full) * 16 + 2 * j + r
+                rows_ref[row : row + 1, 0:TILE] = window[r : r + 1, j * TILE : (j + 1) * TILE]
+    rows = rows_ref[:, 0:TILE]
+    upper = rows.astype(BF16)
+    table_ref[0] = upper
+    table_ref[1] = (rows - upper.astype(F32)).astype(BF16)
+    rows_ref[0:1, TILE:] = jnp.zeros((1, LANES), F32) + base.astype(F32)
 
     def one_hot(row, count):
         rows = lax.broadcasted_iota(jnp.int32, (count, row.shape[1]), 0).astype(F32).astype(BF16)
         match = row.astype(F32).astype(BF16) == rows
         return jnp.where(match, jnp.ones_like(rows), jnp.zeros_like(rows))
 
-    def pick(sky_ref, first, at, width):
+    def pick(first, at, width):
         index = ell_ref[pl.ds(at, width)].reshape(1, width) - base
         span = lax.shift_right_arithmetic(index, 8)
         hot_ell = one_hot(lax.bitwise_and(index, TILE - 1), TILE)
@@ -187,8 +220,8 @@
             here = span == j
             beam_re = jnp.where(here, picked[j * pair : j * pair + full], beam_re)
             beam_im = jnp.where(here, picked[j * pair + full : (j + 1) * pair], beam_im)
-        sky_re = sky_ref[0:1, first : first + width]
-        sky_im = sky_ref[1:2, first : first + width]
+        sky_re = sky_ref[0:1, pl.ds(at, width)]
+        sky_im = sky_ref[1:2, pl.ds(at, width)]
         tiles = width // LANES
         start = first // LANES
 
@@ -230,10 +263,10 @@
                     both = jnp.concatenate([part * row_re, part * row_im], axis=0).astype(BF16)
                     values_ref[top : top + 16, lanes] = both
 
-    def add_chunk(w_ref, sky_ref, at, width):
+    def add_chunk(w_ref, at, width):
         part = min(width, PIECE)
         for first in range(0, width, part):
-            pick(sky_ref, first, at + first, part)
+            pick(first, at + first, part)
             spread(w_ref, first, part)
         hot_col = one_hot(col_ref[pl.ds(at, width)].reshape(1, width), cols)
         sum_ref[...] += lax.dot_general(
@@ -244,27 +277,36 @@
         )
 
     base = rows_ref[0:1, TILE : TILE + 1].astype(jnp.int32)
-    add_chunk(streams[0], streams[1], pl.multiple_of(step * block, block), block)
-
-    @pl.when(step == steps - 1)
-    def _():
-        if tail:
-            add_chunk(streams[2], streams[3], steps * block, tail)
-        share = cycles // shares
-        for half in range(0, cols, LANES):
-            size = min(cols - half, LANES)
-            turn_ref[half // LANES, :, 0:size] = sum_ref[:, half : half + size]
-        for d in range(shares):
-            for i in range(share):
-                t = lax.bitwise_xor(me_ref[0], d) * share + i
-                start = t // 8 * 16 + t % 8
-                for r in range(2):
-                    top = (2 * i + r) * orders
-                    rows = pl.ds(start + r * 8, orders, stride=2 * cycles)
-                    for lane in range(0, cols, LANES):
-                        size = min(cols - lane, LANES)
-                        every = turn_ref[lane // LANES, rows, :]
-                        out_refs[d][top : top + orders, lane : lane + size] = every[:, 0:size]
+
+    def body(i, carry):
+        arrival(i).wait()
+
+        @pl.when(i + 1 < steps)
+        def _():
+            arrival(i + 1).start()
+
+        add_chunk(held_ref.at[lax.rem(i, 2)], pl.multiple_of(i * block, block), block)
+        return carry
+
+    lax.fori_loop(0, steps, body, 0)
+    if tail:
+        last_arrival().wait()
+        add_chunk(last_ref, steps * block, tail)
+    share = cycles // shares
+    for half in range(0, cols, LANES):
+        size = min(cols - half, LANES)
+        turn_ref[half // LANES, :, 0:size] = sum_ref[:, half : half + size]
+    for d in range(shares):
+        for i in range(share):
+            t = lax.bitwise_xor(me_ref[0], d) * share + i
+            start = t // 8 * 16 + t % 8
+            for r in range(2):
+                top = (2 * i + r) * orders
+                rows = pl.ds(start + r * 8, orders, stride=2 * cycles)
+                for lane in range(0, cols, LANES):
+                    size = min(cols - lane, LANES)
+                    every = turn_ref[lane // LANES, rows, :]
+                    out_refs[d][top : top + orders, lane : lane + size] = every[:, 0:size]
 
 
 def column_sums(me, wigner, sky_alm, beam, slot_col, slot_ell, cols, spans, shares):
@@ -277,24 +319,12 @@
     table_rows = spans * 2 * full + 16 * (orders - full)
     whole = pl.BlockSpec(memory_space=pltpu.VMEM)
 
-    def specs(width, at):
-        return [
-            pl.BlockSpec((orders, cycles, width), lambda i: (0, 0, at(i))),
-            pl.BlockSpec((2, width), lambda i: (0, at(i))),
-        ]
-
-    in_specs = [pl.BlockSpec(memory_space=pltpu.SMEM), whole, whole, whole] + specs(block, lambda i: i)
-    operands = [me, slot_col, slot_ell, beam, wigner, sky_alm]
-    if tail:
-        at = slots // tail - 1
-        in_specs += specs(tail, lambda i: at)
-        operands += [wigner, sky_alm]
     out_shape = (rows // shares, cols)
     return pl.pallas_call(
         functools.partial(sums_kernel, (cycles, orders, cols, spans, block, tail, steps, shares)),
-        grid=(steps,),
-        in_specs=in_specs,
-        out_specs=[pl.BlockSpec(out_shape, lambda i: (0, 0))] * shares,
+        in_specs=[pl.BlockSpec(memory_space=pltpu.SMEM)]
+        + [pl.BlockSpec(memory_space=pltpu.HBM)] * 5,
+        out_specs=[whole] * shares,
         scratch_shapes=[
             pltpu.VMEM((rows, cols), F32),
             pltpu.VMEM((rows, block), BF16),
@@ -302,13 +332,18 @@
             pltpu.VMEM((table_rows, TILE + LANES), F32),
             pltpu.VMEM((-(-cols // LANES), rows, LANES), F32),
             pltpu.VMEM((block // LANES, 2 * full + 8 * (orders - full), LANES), F32),
+            pltpu.VMEM((2, orders, cycles, block), BF16),
+            pltpu.VMEM((orders, cycles, max(tail, LANES)), BF16),
+            pltpu.VMEM(slot_col.shape, slot_col.dtype),
+            pltpu.VMEM(slot_ell.shape, slot_ell.dtype),
+            pltpu.VMEM(beam.shape, beam.dtype),
+            pltpu.VMEM(sky_alm.shape, sky_alm.dtype),
+            pltpu.SemaphoreType.DMA((7,)),
         ],
         out_shape=[jax.ShapeDtypeStruct(out_shape, F32)] * shares,
-        compiler_params=pltpu.CompilerParams(
-            dimension_semantics=("arbitrary",), vmem_limit_bytes=60 * 2**20
-        ),
+        compiler_params=pltpu.CompilerParams(vmem_limit_bytes=54784 * 2**10),
         name="column_sums",
-    )(*operands)
+    )(me, slot_col, slot_ell, beam, sky_alm, wigner)
 
 
 def degree_width(degrees, ell_count, blk_count, cols):

time: 55.5 us -> 52.9 us (0.953)
  Pallas kernels: 32.7 us -> 31.3 us
  local copies, waits for them, and re-layouts: 0.89 us -> 0.01 us
    pallas_call x1, Pallas kernels: 29.8 us -> 28.4 us  [column_sums(): pl.pallas_call(functools.partial(sums_kernel, (cycles, orders, cols, span...]
    unnamed x6 -> x4, local copies, waits for them, and re-layouts: 0.89 us -> 0.01 us
  transfers between devices with their start and end apart: 4 -> 4, of which waited for: 2 -> 2; matrix products, arithmetic and copies ran while one was open for 10% -> 11% of each run, Pallas kernels for 0% -> 0%
where the time goes in v4:
time: 52.9 us; the launch traced here: 52.7 us
  Pallas kernels  31.3 us (59%)
  starting transfers between devices  9.45 us (18%)
  waiting for transfers between devices  6.27 us (12%)
  other arithmetic  5.66 us (11%)
    pallas_call x1, Pallas kernels, column_sums(): pl.pallas_call(functools.partial(sums_kernel, (cycles, orders, cols, span...  28.4 us
    all_to_all x1, waiting for transfers between devices, on_device(): lax.all_to_all(fields, 'blk', split_axis=0, concat_axis=0, tiled=True)  5.65 us
    all_to_all x1, starting transfers between devices, on_device(): lax.all_to_all(fields, 'blk', split_axis=0, concat_axis=0, tiled=True)  4.86 us
    ppermute x3, starting transfers between devices, on_device(): lax.ppermute(part, 'ell', [(i, i ^ d) for i in range(ell_count)])  4.59 us
    convert_element_type x1, other arithmetic, halves(): return (upper.astype(BF16), (array - upper).astype(BF16))  4.56 us
    pallas_call x1, Pallas kernels, to_phi(): pl.pallas_call(functools.partial(phi_kernel, cycles), out_shape=jax.Shape...  1.95 us
    sin x1, other arithmetic, waves(): return (jnp.cos(angle), jnp.sin(angle))  1.1 us
  transfers between devices with their start and end apart: 4, of which 2 were waited for; matrix products, arithmetic and copies ran while one was open for 11% of the time, Pallas kernels for 0%

profile of v4, /device:TPU:0, one launch (start us, length us, event | category | flops | bytes accessed | tf_op | source)
XLA Modules:
  0.0 52.7 jit_solution(3594740930773272900)
XLA Ops:
  0.0 0.0 copy-start
  0.0 0.0 copy-start.1
  0.0 28.4 %column_sums.1 = (f32[68,256]{1,0:T(8,128)S(1)}, f32[68,256]{1,0:T(8,128)S(1)}, f32[68,256]{1,0:T(8,128)S(1)}, f32[68,256]{1,0:T(8,128)S(1)}) custom-call(s32[1]{0:T(128)} %bitcast.me_ref, s32[65664]{0:T(1024)} %refs_0_.1, s32[65664]{0:T(1024)} %refs_1_.1, f32[17,2,2048]{2,1,0:T(2,128)} %bitcast.5, f32[2,65664]{1,0:T(2,128)} %refs_3_.1, ...), custom_call_target="tpu_custom_call" | custom-call | tf_op jit(solution)/shard_map/column_sums/pallas_call | solution.py:323
  28.4 3.1 %collective-permute-start = (f32[68,256]{1,0:T(8,128)S(1)}, f32[68,256]{1,0:T(8,128)S(1)}, u32[]{:S(2)}, u32[]{:S(2)}) collective-permute-start(f32[68,256]{1,0:T(8,128)S(1)} %get-tuple-element.10), channel_id=1, source_target_pairs={{0,8},{8,0},{16,24},{24,16},{1,9},{9,1},{17,25},{25,17},{2,10},{10... | collective-permute-start | bytes 208904 | tf_op jit(solution)/shard_map/ppermute | solution.py:379
  31.5 1.5 %collective-permute-start.1 = (f32[68,256]{1,0:T(8,128)S(1)}, f32[68,256]{1,0:T(8,128)S(1)}, u32[]{:S(2)}, u32[]{:S(2)}) collective-permute-start(f32[68,256]{1,0:T(8,128)S(1)} %get-tuple-element.11), channel_id=1, source_target_pairs={{0,16},{8,24},{16,0},{24,8},{1,17},{9,25},{17,1},{25,9},{2,18},{10... | collective-permute-start | bytes 208904 | tf_op jit(solution)/shard_map/ppermute | solution.py:379
  33.0 0.0 collective-permute-start.2
  33.0 0.0 copy-done.1
  33.0 4.6 %fusion.1 = (bf16[128,2048]{1,0:T(8,128)(2,1)S(1)}, bf16[128,2048]{1,0:T(8,128)(2,1)S(1)}, bf16[128,2048]{1,0:T(8,128)(2,1)S(1)}, bf16[128,2048]{1,0:T(8,128)(2,1)S(1)}) fusion(s32[2048]{0:T(1024)S(1)} %copy-done.1), kind=kLoop, calls=%fused_computation.8 | loop fusion | flops 6029312 | bytes 2105344 | tf_op jit(solution)/shard_map/convert_element_type | solution.py:59
  37.6 0.0 collective-permute-done.refs_1_
  37.6 0.0 collective-permute-done.1.refs_2_
  37.6 0.6 %collective-permute-done.2.refs_3_ = f32[68,256]{1,0:T(8,128)S(1)} collective-permute-done((f32[68,256]{1,0:T(8,128)S(1)}, f32[68,256]{1,0:T(8,128)S(1)}, u32[]{:S(2)}, u32[]{:S(2)}) %collective-permute-start.2) | collective-permute-done | bytes 69664 | tf_op jit(solution)/shard_map/ppermute | solution.py:379
  38.2 0.0 copy-done
  38.2 0.9 %psi.1 = f32[128,256]{1,0:T(8,128)} custom-call(f32[128,68]{1,0:T(8,128)S(1)} %copy-done, f32[68,256]{1,0:T(8,128)S(1)} %get-tuple-element.9.refs_0_, f32[68,256]{1,0:T(8,128)S(1)} %collective-permute-done.refs_1_, f32[68,256]{1,0:T(8,128)S(1)} %collective-permute-done.1.refs_2_, f32[68,256]{1,0:T(8,128)S(1)} %collective-permute-done.2.refs_3_), custom_call_target="tpu_custom_call" | custom-call | tf_op jit(solution)/shard_map/psi/pallas_call | solution.py:48
  39.1 4.9 %all-to-all-start = ((f32[8,16,256]{2,1,0:T(8,128)}), f32[8,16,256]{2,1,0:T(8,128)S(1)}, u32[]{:S(2)}, u32[]{:S(2)}) async-start(f32[8,16,256]{2,1,0:T(8,128)} %bitcast.3), calls=%async_computation | async-start | bytes 262144 | tf_op jit(solution)/shard_map/all_to_all | solution.py:383
  44.0 1.1 %fusion.12 = (f32[32,2048]{1,0:T(8,128)S(1)}, f32[32,2048]{1,0:T(8,128)S(1)}) fusion(s32[2048]{0:T(1024)S(1)} %copy-done.1, s32[32]{0:T(128)S(1)} %iota_multiply_fusion), kind=kLoop, calls=%fused_computation.25 | loop fusion | flops 917504 | bytes 532608 | tf_op jit(solution)/shard_map/sin | solution.py:66
  45.1 5.6 %all-to-all-done.fields_ref = f32[8,16,256]{2,1,0:T(8,128)S(1)} async-done(((f32[8,16,256]{2,1,0:T(8,128)}), f32[8,16,256]{2,1,0:T(8,128)S(1)}, u32[]{:S(2)}, u32[]{:S(2)}) %all-to-all-start) | async-done | bytes 131104 | tf_op jit(solution)/shard_map/all_to_all | solution.py:383
  50.7 1.9 %phi.1 = f32[2,4,4096]{2,1,0:T(4,128)} custom-call(f32[8,16,256]{2,1,0:T(8,128)S(1)} %all-to-all-done.fields_ref, f32[32,2048]{1,0:T(8,128)S(1)} %get-tuple-element.14.cos_ref, f32[32,2048]{1,0:T(8,128)S(1)} %get-tuple-element.13.sin_ref, bf16[128,2048]{1,0:T(8,128)(2,1)S(1)} %get-tuple-element.18.ch_ref, bf16[128,2048]{1,0:T(8,128)(2,1)S(1)} %get-tuple-element.16.cl_ref, ...), custom_call_target="tpu_custom_call" | custom-call | tf_op jit(solution)/shard_map/phi/pallas_call | solution.py:120
  (1 shorter events, 0.0 us)
Async XLA Ops:
  0.0 38.2 %copy-start = (f32[128,68]{1,0:T(8,128)S(1)}, f32[128,68]{1,0:T(8,128)}, u32[]{:S(2)}) copy-start(f32[128,68]{1,0:T(8,128)} %constant.35.clone.matrix_ref) | copy-start | bytes 104452
  0.0 33.0 %copy-start.1 = (s32[2048]{0:T(1024)S(1)}, s32[2048]{0:T(1024)}, u32[]{:S(2)}) copy-start(s32[2048]{0:T(1024)} %param.12) | copy-start | bytes 24580
  28.4 9.2 %collective-permute-start = (f32[68,256]{1,0:T(8,128)S(1)}, f32[68,256]{1,0:T(8,128)S(1)}, u32[]{:S(2)}, u32[]{:S(2)}) collective-permute-start(f32[68,256]{1,0:T(8,128)S(1)} %get-tuple-element.10), channel_id=1, source_target_pairs={{0,8},{8,0},{16,24},{24,16},{1,9},{9,1},{17,25},{25,17},{2,10},{10... | collective-permute-start | bytes 208904 | tf_op jit(solution)/shard_map/ppermute | solution.py:379
  31.5 6.1 %collective-permute-start.1 = (f32[68,256]{1,0:T(8,128)S(1)}, f32[68,256]{1,0:T(8,128)S(1)}, u32[]{:S(2)}, u32[]{:S(2)}) collective-permute-start(f32[68,256]{1,0:T(8,128)S(1)} %get-tuple-element.11), channel_id=1, source_target_pairs={{0,16},{8,24},{16,0},{24,8},{1,17},{9,25},{17,1},{25,9},{2,18},{10... | collective-permute-start | bytes 208904 | tf_op jit(solution)/shard_map/ppermute | solution.py:379
  33.0 5.3 %collective-permute-start.2 = (f32[68,256]{1,0:T(8,128)S(1)}, f32[68,256]{1,0:T(8,128)S(1)}, u32[]{:S(2)}, u32[]{:S(2)}) collective-permute-start(f32[68,256]{1,0:T(8,128)S(1)} %get-tuple-element.12), channel_id=1, source_target_pairs={{0,24},{8,16},{16,8},{24,0},{1,25},{9,17},{17,9},{25,1},{2,26},{10... | collective-permute-start | bytes 208904 | tf_op jit(solution)/shard_map/ppermute | solution.py:379
  39.1 11.6 %all-to-all-start = ((f32[8,16,256]{2,1,0:T(8,128)}), f32[8,16,256]{2,1,0:T(8,128)S(1)}, u32[]{:S(2)}, u32[]{:S(2)}) async-start(f32[8,16,256]{2,1,0:T(8,128)} %bitcast.3), calls=%async_computation | async-start | bytes 262144 | tf_op jit(solution)/shard_map/all_to_all | solution.py:383

commit v5 on v4

--- a/solution.py
+++ b/solution.py
@@ -33,24 +33,31 @@
     return matrix.reshape(blks * cycles * 2 * samples, cycles * orders * 2)
 
 
-def psi_kernel(matrix_ref, *refs):
+def psi_kernel(high_ref, low_ref, *refs):
     total = refs[0][...]
     for part_ref in refs[1:-1]:
         total = total + part_ref[...]
-    refs[-1][...] = jnp.dot(
-        matrix_ref[...], total, precision=lax.Precision.HIGHEST, preferred_element_type=F32
-    )
+    upper = total.astype(BF16)
+    lower = (total - upper.astype(F32)).astype(BF16)
+
+    def product(left, right):
+        return jnp.dot(left, right, preferred_element_type=F32)
+
+    high = high_ref[...]
+    refs[-1][...] = product(high, upper) + (product(high, lower) + product(low_ref[...], upper))
 
 
 def to_psi(parts, blks, cycles, orders):
     matrix = psi_matrix(blks, cycles, orders)
+    upper = matrix.astype(BF16)
+    lower = (matrix - upper.astype(np.float32)).astype(BF16)
     rows, cols = matrix.shape[0], parts[0].shape[1]
     out = pl.pallas_call(
         psi_kernel,
         out_shape=jax.ShapeDtypeStruct((rows, cols), F32),
         compiler_params=pltpu.CompilerParams(vmem_limit_bytes=16 * 2**20),
         name="psi",
-    )(jnp.asarray(matrix), *parts)
+    )(jnp.asarray(upper), jnp.asarray(lower), *parts)
     return out.reshape(blks, rows // blks, cols)
 
 
@@ -171,8 +178,9 @@
     def lowest_degree():
         def fold(at, width, low):
             where = pl.ds(at, width)
-            col = col_ref[where].reshape(1, width)
-            ell = ell_ref[where].reshape(1, width).astype(F32)
+            shape = (width // LANES, LANES)
+            col = col_ref[where].reshape(shape)
+            ell = ell_ref[where].reshape(shape).astype(F32)
             return jnp.minimum(low, jnp.min(jnp.where(col >= 0, ell, float(degrees))))
 
         low = float(degrees)
@@ -374,12 +382,13 @@
         spans,
         ell_count,
     )
-    tables = phi_tables(order_of_column, 2 * degree_count)
     parts = [
         part if d == 0 else lax.ppermute(part, "ell", [(i, i ^ d) for i in range(ell_count)])
         for d, part in enumerate(parts)
     ]
     fields = to_psi(parts, blk_count, cycle_share, order_count)
+    fields, order_of_column = lax.optimization_barrier((fields, order_of_column))
+    tables = phi_tables(order_of_column, 2 * degree_count)
     fields = lax.all_to_all(fields, "blk", split_axis=0, concat_axis=0, tiled=True)
     return to_phi(fields, tables, cycle_share)
 

time: 52.9 us -> 52.9 us (level)
    all_to_all x1, waiting for transfers between devices: 5.65 us -> 1.06 us  [on_device(): lax.all_to_all(fields, 'blk', split_axis=0, concat_axis=0, tiled=True)]
    ppermute x3, waiting for transfers between devices: 0.62 us -> 5.21 us  [on_device(): lax.ppermute(part, 'ell', [(i, i ^ d) for i in range(ell_count)])]
  transfers between devices with their start and end apart: 4 -> 4, of which waited for: 2 -> 4; matrix products, arithmetic and copies ran while one was open for 11% -> 11% of each run, Pallas kernels for 0% -> 0%
where the time goes in v5:
time: 52.9 us; the launch traced here: 52.6 us
  Pallas kernels  31.1 us (59%)
  starting transfers between devices  9.49 us (18%)
  waiting for transfers between devices  6.26 us (12%)
  other arithmetic  5.68 us (11%)
    pallas_call x1, Pallas kernels, column_sums(): pl.pallas_call(functools.partial(sums_kernel, (cycles, orders, cols, span...  28.3 us
    ppermute x3, waiting for transfers between devices, on_device(): lax.ppermute(part, 'ell', [(i, i ^ d) for i in range(ell_count)])  5.21 us
    all_to_all x1, starting transfers between devices, on_device(): lax.all_to_all(fields, 'blk', split_axis=0, concat_axis=0, tiled=True)  4.88 us
    ppermute x3, starting transfers between devices, on_device(): lax.ppermute(part, 'ell', [(i, i ^ d) for i in range(ell_count)])  4.61 us
    convert_element_type x1, other arithmetic, halves(): return (upper.astype(BF16), (array - upper).astype(BF16))  4.58 us
    pallas_call x1, Pallas kernels, to_phi(): pl.pallas_call(functools.partial(phi_kernel, cycles), out_shape=jax.Shape...  1.95 us
    sin x1, other arithmetic, waves(): return (jnp.cos(angle), jnp.sin(angle))  1.1 us
  transfers between devices with their start and end apart: 4, of which 4 were waited for; matrix products, arithmetic and copies ran while one was open for 11% of the time, Pallas kernels for 0%

profile of v5, /device:TPU:0, one launch (start us, length us, event | category | flops | bytes accessed | tf_op | source)
XLA Modules:
  0.0 52.6 jit_solution(3833262295409530143)
XLA Ops:
  0.0 0.0 copy-start
  0.0 0.0 copy-start.1
  0.0 0.0 copy-start.2
  0.0 28.3 %column_sums.1 = (f32[68,256]{1,0:T(8,128)S(1)}, f32[68,256]{1,0:T(8,128)S(1)}, f32[68,256]{1,0:T(8,128)S(1)}, f32[68,256]{1,0:T(8,128)S(1)}) custom-call(s32[1]{0:T(128)} %bitcast.me_ref, s32[65664]{0:T(1024)} %refs_0_.1, s32[65664]{0:T(1024)} %refs_1_.1, f32[17,2,2048]{2,1,0:T(2,128)} %bitcast.5, f32[2,65664]{1,0:T(2,128)} %refs_3_.1, ...), custom_call_target="tpu_custom_call" | custom-call | tf_op jit(solution)/shard_map/column_sums/pallas_call | solution.py:331
  28.3 3.1 %collective-permute-start = (f32[68,256]{1,0:T(8,128)S(1)}, f32[68,256]{1,0:T(8,128)S(1)}, u32[]{:S(2)}, u32[]{:S(2)}) collective-permute-start(f32[68,256]{1,0:T(8,128)S(1)} %get-tuple-element.12), channel_id=1, source_target_pairs={{0,8},{8,0},{16,24},{24,16},{1,9},{9,1},{17,25},{25,17},{2,10},{10... | collective-permute-start | bytes 208904 | tf_op jit(solution)/shard_map/ppermute | solution.py:386
  31.4 1.5 %collective-permute-start.1 = (f32[68,256]{1,0:T(8,128)S(1)}, f32[68,256]{1,0:T(8,128)S(1)}, u32[]{:S(2)}, u32[]{:S(2)}) collective-permute-start(f32[68,256]{1,0:T(8,128)S(1)} %get-tuple-element.13), channel_id=1, source_target_pairs={{0,16},{8,24},{16,0},{24,8},{1,17},{9,25},{17,1},{25,9},{2,18},{10... | collective-permute-start | bytes 208904 | tf_op jit(solution)/shard_map/ppermute | solution.py:386
  32.9 0.0 collective-permute-start.2
  32.9 1.0 %collective-permute-done.refs_1_ = f32[68,256]{1,0:T(8,128)S(1)} collective-permute-done((f32[68,256]{1,0:T(8,128)S(1)}, f32[68,256]{1,0:T(8,128)S(1)}, u32[]{:S(2)}, u32[]{:S(2)}) %collective-permute-start) | collective-permute-done | bytes 69664 | tf_op jit(solution)/shard_map/ppermute | solution.py:386
  33.9 1.8 %collective-permute-done.1.refs_2_ = f32[68,256]{1,0:T(8,128)S(1)} collective-permute-done((f32[68,256]{1,0:T(8,128)S(1)}, f32[68,256]{1,0:T(8,128)S(1)}, u32[]{:S(2)}, u32[]{:S(2)}) %collective-permute-start.1) | collective-permute-done | bytes 69664 | tf_op jit(solution)/shard_map/ppermute | solution.py:386
  35.8 2.4 %collective-permute-done.2.refs_3_ = f32[68,256]{1,0:T(8,128)S(1)} collective-permute-done((f32[68,256]{1,0:T(8,128)S(1)}, f32[68,256]{1,0:T(8,128)S(1)}, u32[]{:S(2)}, u32[]{:S(2)}) %collective-permute-start.2) | collective-permute-done | bytes 69664 | tf_op jit(solution)/shard_map/ppermute | solution.py:386
  38.2 0.0 copy-done
  38.2 0.0 copy-done.1
  38.2 0.9 %psi.1 = f32[128,256]{1,0:T(8,128)} custom-call(bf16[128,68]{1,0:T(8,128)(2,1)S(1)} %copy-done.1, bf16[128,68]{1,0:T(8,128)(2,1)S(1)} %copy-done, f32[68,256]{1,0:T(8,128)S(1)} %get-tuple-element.11.refs_0_, f32[68,256]{1,0:T(8,128)S(1)} %collective-permute-done.refs_1_, f32[68,256]{1,0:T(8,128)S(1)} %collective-permute-done.1.refs_2_, ...), custom_call_target="tpu_custom_call" | custom-call | tf_op jit(solution)/shard_map/psi/pallas_call | solution.py:55
  39.0 4.9 %all-to-all-start = ((f32[8,16,256]{2,1,0:T(8,128)}), f32[8,16,256]{2,1,0:T(8,128)S(1)}, u32[]{:S(2)}, u32[]{:S(2)}) async-start(f32[8,16,256]{2,1,0:T(8,128)} %bitcast.3), calls=%async_computation | async-start | bytes 262144 | tf_op jit(solution)/shard_map/all_to_all | solution.py:392
  43.9 0.0 copy-done.2
  43.9 4.6 %fusion.1 = (bf16[128,2048]{1,0:T(8,128)(2,1)S(1)}, bf16[128,2048]{1,0:T(8,128)(2,1)S(1)}, bf16[128,2048]{1,0:T(8,128)(2,1)S(1)}, bf16[128,2048]{1,0:T(8,128)(2,1)S(1)}) fusion(s32[2048]{0:T(1024)S(1)} %copy-done.2), kind=kLoop, calls=%fused_computation.8 | loop fusion | flops 6029312 | bytes 2105344 | tf_op jit(solution)/shard_map/convert_element_type | solution.py:66
  48.5 1.1 %fusion.12 = (f32[32,2048]{1,0:T(8,128)S(1)}, f32[32,2048]{1,0:T(8,128)S(1)}) fusion(s32[2048]{0:T(1024)S(1)} %copy-done.2, s32[32]{0:T(128)S(1)} %iota_multiply_fusion), kind=kLoop, calls=%fused_computation.25 | loop fusion | flops 917504 | bytes 532608 | tf_op jit(solution)/shard_map/sin | solution.py:73
  49.6 1.1 %all-to-all-done.fields_ref = f32[8,16,256]{2,1,0:T(8,128)S(1)} async-done(((f32[8,16,256]{2,1,0:T(8,128)}), f32[8,16,256]{2,1,0:T(8,128)S(1)}, u32[]{:S(2)}, u32[]{:S(2)}) %all-to-all-start) | async-done | bytes 131104 | tf_op jit(solution)/shard_map/all_to_all | solution.py:392
  50.7 2.0 %phi.1 = f32[2,4,4096]{2,1,0:T(4,128)} custom-call(f32[8,16,256]{2,1,0:T(8,128)S(1)} %all-to-all-done.fields_ref, f32[32,2048]{1,0:T(8,128)S(1)} %get-tuple-element.18.cos_ref, f32[32,2048]{1,0:T(8,128)S(1)} %get-tuple-element.17.sin_ref, bf16[128,2048]{1,0:T(8,128)(2,1)S(1)} %get-tuple-element.22.ch_ref, bf16[128,2048]{1,0:T(8,128)(2,1)S(1)} %get-tuple-element.20.cl_ref, ...), custom_call_target="tpu_custom_call" | custom-call | tf_op jit(solution)/shard_map/phi/pallas_call | solution.py:127
  (1 shorter events, 0.0 us)
Async XLA Ops:
  0.0 38.2 %copy-start = (bf16[128,68]{1,0:T(8,128)(2,1)S(1)}, bf16[128,68]{1,0:T(8,128)(2,1)}, u32[]{:S(2)}) copy-start(bf16[128,68]{1,0:T(8,128)(2,1)} %constant.38.clone.low_ref) | copy-start | bytes 52228
  0.0 38.2 %copy-start.1 = (bf16[128,68]{1,0:T(8,128)(2,1)S(1)}, bf16[128,68]{1,0:T(8,128)(2,1)}, u32[]{:S(2)}) copy-start(bf16[128,68]{1,0:T(8,128)(2,1)} %constant.37.clone.high_ref) | copy-start | bytes 52228
  0.0 43.9 %copy-start.2 = (s32[2048]{0:T(1024)S(1)}, s32[2048]{0:T(1024)}, u32[]{:S(2)}) copy-start(s32[2048]{0:T(1024)} %param.13) | copy-start | bytes 24580
  28.3 5.6 %collective-permute-start = (f32[68,256]{1,0:T(8,128)S(1)}, f32[68,256]{1,0:T(8,128)S(1)}, u32[]{:S(2)}, u32[]{:S(2)}) collective-permute-start(f32[68,256]{1,0:T(8,128)S(1)} %get-tuple-element.12), channel_id=1, source_target_pairs={{0,8},{8,0},{16,24},{24,16},{1,9},{9,1},{17,25},{25,17},{2,10},{10... | collective-permute-start | bytes 208904 | tf_op jit(solution)/shard_map/ppermute | solution.py:386
  31.4 4.4 %collective-permute-start.1 = (f32[68,256]{1,0:T(8,128)S(1)}, f32[68,256]{1,0:T(8,128)S(1)}, u32[]{:S(2)}, u32[]{:S(2)}) collective-permute-start(f32[68,256]{1,0:T(8,128)S(1)} %get-tuple-element.13), channel_id=1, source_target_pairs={{0,16},{8,24},{16,0},{24,8},{1,17},{9,25},{17,1},{25,9},{2,18},{10... | collective-permute-start | bytes 208904 | tf_op jit(solution)/shard_map/ppermute | solution.py:386
  32.9 5.3 %collective-permute-start.2 = (f32[68,256]{1,0:T(8,128)S(1)}, f32[68,256]{1,0:T(8,128)S(1)}, u32[]{:S(2)}, u32[]{:S(2)}) collective-permute-start(f32[68,256]{1,0:T(8,128)S(1)} %get-tuple-element.14), channel_id=1, source_target_pairs={{0,24},{8,16},{16,8},{24,0},{1,25},{9,17},{17,9},{25,1},{2,26},{10... | collective-permute-start | bytes 208904 | tf_op jit(solution)/shard_map/ppermute | solution.py:386
  39.0 11.6 %all-to-all-start = ((f32[8,16,256]{2,1,0:T(8,128)}), f32[8,16,256]{2,1,0:T(8,128)S(1)}, u32[]{:S(2)}, u32[]{:S(2)}) async-start(f32[8,16,256]{2,1,0:T(8,128)} %bitcast.3), calls=%async_computation | async-start | bytes 262144 | tf_op jit(solution)/shard_map/all_to_all | solution.py:392
